TPU v7x, 32 devices: a whole 2x2x4 slice. The times are simulated.
32 devices in a mesh: rep: 4 (over x, core), grp: 8 (over z, y).
Axes of the slice: x: 2, y: 2, z: 4, core: 2. Of those that a mesh axis runs over, the one named last changes fastest.
Arguments:
- tokens: float32 [8192, 1088], P(('rep', 'grp')), may hold values from -6 to 6
- document_lengths: int32 [32, 8], P(('rep', 'grp')), may hold values from 0 to 256, as said below
- cotangent: float32 [8192, 1088], P(('rep', 'grp')), may hold values from -6 to 6
- first_gain: bfloat16 [1088], P('grp'), may hold values from 0.25 to 1.75
- first_shift: bfloat16 [1088], P('grp'), may hold values from -3 to 3
- attention_in: bfloat16 [1088, 3264], P(None, 'grp'), may hold values from -2 to 2
- query_bias: bfloat16 [1088], P('grp'), may hold values from -3 to 3
- value_bias: bfloat16 [1088], P('grp'), may hold values from -3 to 3
- attention_out: bfloat16 [1088, 1088], P(None, 'grp'), may hold values from -0.75 to 0.75
- output_bias: bfloat16 [1088], P('grp'), may hold values from -3 to 3
- second_gain: bfloat16 [1088], P('grp'), may hold values from 0.25 to 1.75
- second_shift: bfloat16 [1088], P('grp'), may hold values from -3 to 3
- expand_weight: bfloat16 [1088, 4352], P(None, 'grp'), may hold values from -0.1875 to 0.1875
- expand_bias: bfloat16 [4352], P('grp'), may hold values from -3 to 3
- contract_weight: bfloat16 [4352, 1088], P(None, 'grp'), may hold values from -0.09375 to 0.09375
- contract_bias: bfloat16 [1088], P('grp'), may hold values from -3 to 3
Outputs:
- block_output: float32 [8192, 1088], P(('rep', 'grp'))
- tokens_gradient: float32 [8192, 1088], P(('rep', 'grp'))
- first_gain_gradient: float32 [1088], P('grp')
- first_shift_gradient: float32 [1088], P('grp')
- attention_in_gradient: float32 [1088, 3264], P(None, 'grp')
- query_bias_gradient: float32 [1088], P('grp')
- value_bias_gradient: float32 [1088], P('grp')
- attention_out_gradient: float32 [1088, 1088], P(None, 'grp')
- output_bias_gradient: float32 [1088], P('grp')
- second_gain_gradient: float32 [1088], P('grp')
- second_shift_gradient: float32 [1088], P('grp')
- expand_weight_gradient: float32 [1088, 4352], P(None, 'grp')
- expand_bias_gradient: float32 [4352], P('grp')
- contract_weight_gradient: float32 [4352, 1088], P(None, 'grp')
- contract_bias_gradient: float32 [1088], P('grp')
Inputs may be any that keep to these rules, and one draw needn't show every extreme that they name: `document_lengths`: row r lists, in slot order, the lengths of up to 8 documents packed from the first of device r's 256 slots; a row sums to at least 64 and at most 256, some lengths are zero, and in every draw one row is a single document filling all 256 slots.
All inputs are finite; a program needn't handle non-finite values.
Results may differ from a plain program's by a relative error of at most 0.012.
Values may be sent and summed in bfloat16 or wider, within the bound.
A program may use at most 320 MiB of HBM per device.

v0:
```python
import jax
import jax.numpy as jnp
from jax import lax
from jax.sharding import PartitionSpec as P

D = 1088
H = 17
HD = 64


EPSILON = 1e-05
MASKED = -1e30


def matmul(left, right):
    return jnp.dot(left, right, preferred_element_type=jnp.float32)


def product(form, left, right):
    return jnp.einsum(form, left, right, preferred_element_type=jnp.float32)


def layer_norm(values, gain, shift):
    center = values - jnp.mean(values, axis=-1, keepdims=True)
    inverse = lax.rsqrt(jnp.mean(center * center, axis=-1, keepdims=True) + EPSILON)
    normed = center * inverse
    return (normed, inverse, normed * gain.astype(jnp.float32) + shift.astype(jnp.float32))


def norm_back(upstream, normed, inverse, gain):
    scaled = upstream * gain.astype(jnp.float32)
    return inverse * (
        scaled
        - jnp.mean(scaled, axis=-1, keepdims=True)
        - normed * jnp.mean(scaled * normed, axis=-1, keepdims=True)
    )


def document_layout(lengths, count):
    ends = jnp.cumsum(lengths)
    slots = jnp.arange(count, dtype=jnp.int32)
    number = jnp.sum((slots[:, None] >= ends[None, :]).astype(jnp.int32), axis=1)
    valid = slots < ends[-1]
    labels = jnp.where(valid, number, lengths.shape[0] + slots)
    return (valid, labels)


def block_scores(query, keyset, labels, lower, upper):
    positions = jnp.arange(upper, dtype=jnp.int32)
    allowed = (positions[None, :] <= positions[lower:upper, None]) & (
        labels[None, :upper] == labels[lower:upper, None]
    )
    raw = product("qhd,khd->hqk", query, keyset) * HD ** (-0.5)
    return jnp.where(allowed[None, :, :], raw, MASKED)


def attend_forward(query, keyset, valueset, labels):
    count = query.shape[0]
    span = min(count, 512)
    scores = block_scores(query, keyset, labels, 0, span)
    peak = jnp.max(scores, axis=-1, keepdims=True)
    logsum = peak + jnp.log(jnp.sum(jnp.exp(scores - peak), axis=-1, keepdims=True))
    weights = jnp.exp(scores - logsum).astype(jnp.bfloat16)
    outputs = product("hqk,khd->qhd", weights, valueset)
    totals = logsum[:, :, 0]
    return (outputs, totals)


def attend_backward(query, keyset, valueset, labels, logsum, upstream, attended):
    count = query.shape[0]
    span = min(count, 512)
    delta = jnp.sum(upstream.astype(jnp.float32) * attended.astype(jnp.float32), axis=-1).T
    key_grad = jnp.zeros(keyset.shape, jnp.float32)
    value_grad = jnp.zeros(valueset.shape, jnp.float32)
    scores = block_scores(query, keyset, labels, 0, span)
    probability = jnp.exp(scores - logsum[:, 0:span, None])
    weights = probability.astype(jnp.bfloat16)
    flow = product("qhd,khd->hqk", upstream, valueset)
    slope = (probability * (flow - delta[:, 0:span, None]) * HD ** (-0.5)).astype(jnp.bfloat16)
    query_parts = product("hqk,khd->qhd", slope, keyset)
    key_grad = key_grad.at[:span].add(product("hqk,qhd->khd", slope, query))
    value_grad = value_grad.at[:span].add(product("hqk,qhd->khd", weights, upstream))
    return (query_parts, key_grad, value_grad)


def split_both(left, right, rep_count, grp_count):
    count = left.shape[0]
    left_blocks = left.reshape(count, rep_count, left.shape[1] // rep_count)
    right_blocks = right.reshape(count, grp_count, right.shape[1] // grp_count)
    term = jnp.einsum(
        "tri,tgj->rgij", left_blocks, right_blocks, preferred_element_type=jnp.float32
    )
    return term.reshape(rep_count * grp_count, left_blocks.shape[2], right_blocks.shape[2])


def per_device(
    tokens,
    document_lengths,
    cotangent,
    first_gain,
    first_shift,
    attention_in,
    query_bias,
    value_bias,
    attention_out,
    output_bias,
    second_gain,
    second_shift,
    expand_weight,
    expand_bias,
    contract_weight,
    contract_bias,
):
    count = tokens.shape[0]
    valid, labels = document_layout(document_lengths[0], count)
    gathered_in, gathered_out, gain_one, shift_one, bias_query, bias_value, bias_output = (
        lax.all_gather(attention_in, "grp", axis=1, tiled=True),
        lax.all_gather(attention_out, "grp", axis=1, tiled=True),
        lax.all_gather(first_gain, "grp", axis=0, tiled=True),
        lax.all_gather(first_shift, "grp", axis=0, tiled=True),
        lax.all_gather(query_bias, "grp", axis=0, tiled=True),
        lax.all_gather(value_bias, "grp", axis=0, tiled=True),
        lax.all_gather(output_bias, "grp", axis=0, tiled=True),
    )
    normed_one, inverse_one, hidden_one = layer_norm(tokens, gain_one, shift_one)
    hidden_one = hidden_one.astype(jnp.bfloat16)
    bias_all = jnp.concatenate(
        [
            bias_query.astype(jnp.float32),
            jnp.zeros((D,), jnp.float32),
            bias_value.astype(jnp.float32),
        ]
    )
    projected = (matmul(hidden_one, gathered_in) + bias_all).astype(jnp.bfloat16)
    heads = projected.reshape(count, 3, H, HD)
    query = heads[:, 0]
    keyset = heads[:, 1]
    valueset = heads[:, 2]
    mixed, logsum = attend_forward(query, keyset, valueset, labels)
    attended = mixed.astype(jnp.bfloat16)
    flat_attended = attended.reshape(count, D)
    residual = tokens + matmul(flat_attended, gathered_out) + bias_output.astype(jnp.float32)
    expand_full, contract_full, gain_two, shift_two, bias_expand, bias_contract = (
        lax.all_gather(expand_weight, "grp", axis=1, tiled=True),
        lax.all_gather(contract_weight, "grp", axis=1, tiled=True),
        lax.all_gather(second_gain, "grp", axis=0, tiled=True),
        lax.all_gather(second_shift, "grp", axis=0, tiled=True),
        lax.all_gather(expand_bias, "grp", axis=0, tiled=True),
        lax.all_gather(contract_bias, "grp", axis=0, tiled=True),
    )
    normed_two, inverse_two, hidden_two = layer_norm(residual, gain_two, shift_two)
    hidden_two = hidden_two.astype(jnp.bfloat16)
    before = matmul(hidden_two, expand_full) + bias_expand.astype(jnp.float32)
    activated = jax.nn.gelu(before).astype(jnp.bfloat16)
    output = residual + matmul(activated, contract_full) + bias_contract.astype(jnp.float32)
    live = valid[:, None]
    block_output = jnp.where(live, output, 0.0)
    expand_full, contract_full, gain_two = (
        lax.all_gather(expand_weight, "grp", axis=1, tiled=True),
        lax.all_gather(contract_weight, "grp", axis=1, tiled=True),
        lax.all_gather(second_gain, "grp", axis=0, tiled=True),
    )
    start = jnp.where(live, cotangent, 0.0)
    start_low = start.astype(jnp.bfloat16)
    _, gelu_back = jax.vjp(jax.nn.gelu, before)
    back_before = gelu_back(matmul(start_low, contract_full.T))[0]
    back_before_low = back_before.astype(jnp.bfloat16)
    back_hidden_two = matmul(back_before_low, expand_full.T)
    back_residual = start + norm_back(back_hidden_two, normed_two, inverse_two, gain_two)
    back_residual_low = back_residual.astype(jnp.bfloat16)
    gathered_in, gathered_out, gain_one = (
        lax.all_gather(attention_in, "grp", axis=1, tiled=True),
        lax.all_gather(attention_out, "grp", axis=1, tiled=True),
        lax.all_gather(first_gain, "grp", axis=0, tiled=True),
    )
    back_attended = (
        matmul(back_residual_low, gathered_out.T).astype(jnp.bfloat16).reshape(count, H, HD)
    )
    back_query, back_key, back_value = attend_backward(
        query, keyset, valueset, labels, logsum, back_attended, attended
    )
    back_query = back_query.reshape(count, D)
    back_value = back_value.reshape(count, D)
    back_projected = jnp.concatenate([back_query, back_key.reshape(count, D), back_value], axis=1)
    back_projected_low = back_projected.astype(jnp.bfloat16)
    back_hidden_one = matmul(back_projected_low, gathered_in.T)
    tokens_gradient = back_residual + norm_back(back_hidden_one, normed_one, inverse_one, gain_one)
    vectors = (
        jnp.sum(back_hidden_one * normed_one, axis=0),
        jnp.sum(back_hidden_one, axis=0),
        jnp.sum(back_query, axis=0),
        jnp.sum(back_value, axis=0),
        jnp.sum(back_residual, axis=0),
        jnp.sum(back_hidden_two * normed_two, axis=0),
        jnp.sum(back_hidden_two, axis=0),
        jnp.sum(back_before, axis=0),
        jnp.sum(start, axis=0),
    )
    pairs = (
        (hidden_one, back_projected_low),
        (flat_attended, back_residual_low),
        (hidden_two, back_before_low),
        (activated, start_low),
    )
    rep_count = lax.axis_size("rep")
    grp_count = lax.axis_size("grp")
    blocks = tuple((split_both(left, right, rep_count, grp_count) for left, right in pairs))
    owned = (
        lax.psum_scatter(blocks[0], ("rep", "grp"), scatter_dimension=0, tiled=True),
        lax.psum_scatter(blocks[1], ("rep", "grp"), scatter_dimension=0, tiled=True),
        lax.psum_scatter(blocks[2], ("rep", "grp"), scatter_dimension=0, tiled=True),
        lax.psum_scatter(blocks[3], ("rep", "grp"), scatter_dimension=0, tiled=True),
    )
    spread = (
        lax.all_gather(owned[0], "rep", axis=0, tiled=True),
        lax.all_gather(owned[1], "rep", axis=0, tiled=True),
        lax.all_gather(owned[2], "rep", axis=0, tiled=True),
        lax.all_gather(owned[3], "rep", axis=0, tiled=True),
    )
    matrices = [part.reshape(part.shape[0] * part.shape[1], part.shape[2]) for part in spread]
    summed = lax.psum(
        (
            vectors[0],
            vectors[1],
            vectors[2],
            vectors[3],
            vectors[4],
            vectors[5],
            vectors[6],
            vectors[7],
            vectors[8],
        ),
        ("rep", "grp"),
    )
    place = lax.axis_index("grp")
    shares = [
        lax.dynamic_slice_in_dim(
            total, place * (total.shape[0] // grp_count), total.shape[0] // grp_count
        )
        for total in summed
    ]
    return (
        block_output,
        tokens_gradient,
        shares[0],
        shares[1],
        matrices[0],
        shares[2],
        shares[3],
        matrices[1],
        shares[4],
        shares[5],
        shares[6],
        matrices[2],
        shares[7],
        matrices[3],
        shares[8],
    )


def solution(mesh):
    return jax.shard_map(
        per_device,
        mesh=mesh,
        in_specs=(
            P(("rep", "grp"), None),
            P(("rep", "grp"), None),
            P(("rep", "grp"), None),
            P("grp"),
            P("grp"),
            P(None, "grp"),
            P("grp"),
            P("grp"),
            P(None, "grp"),
            P("grp"),
            P("grp"),
            P("grp"),
            P(None, "grp"),
            P("grp"),
            P(None, "grp"),
            P("grp"),
        ),
        out_specs=(
            P(("rep", "grp"), None),
            P(("rep", "grp"), None),
            P("grp"),
            P("grp"),
            P(None, "grp"),
            P("grp"),
            P("grp"),
            P(None, "grp"),
            P("grp"),
            P("grp"),
            P("grp"),
            P(None, "grp"),
            P("grp"),
            P(None, "grp"),
            P("grp"),
        ),
        check_vma=False,
    )
```

profile of v0, /device:TPU:0, one launch (start us, length us, event | category | flops | bytes accessed | tf_op | source)
XLA Modules:
  0.0 1769.5 jit_solution(3784689904117414297)
XLA Ops:
  7.4 0.7 all-gather.8.cloned.1.call-update
  8.1 0.7 all-gather.10.cloned.1.call-update
  8.8 0.7 all-gather.14.cloned.1.call-update
  15.1 42.2 %all-reduce.12 = (bf16[1088]{0:T(1024)(128)(2,1)S(1)}, bf16[1088]{0:T(1024)(128)(2,1)S(1)}, bf16[1088]{0:T(1024)(128)(2,1)S(1)}, bf16[1088]{0:T(1024)(128)(2,1)S...) all-reduce(bf16[1088]{0:T(1024)(128)(2,1)S(1)} %dynamic-update-slic, ...), channel_id=1, replica_groups=mesh['rep'=4,'grp'=8] {'grp'}, use_global_device_ids=true, to_apply=%add.2 | all-reduce | flops 13056 | bytes 52224
  57.6 0.6 iota_compare_fusion.2
  58.5 0.6 add_select_fusion
  59.8 68.2 %all-gather.8.cloned.1.call-done = bf16[1088,3264]{0,1:T(8,128)(2,1)} async-done(((bf16[1088,408]{0,1:T(8,128)(2,1)}), bf16[1088,3264]{0,1:T(8,128)(2,1)}) %all-gather.8.cloned.1.call-update) | async-done | bytes 7102480 | tf_op jit(solution)/shard_map/all_gather | solution.py:117
  128.0 5.5 fusion
  133.5 0.9 fusion.8
  134.4 0.9 exponential_reduce_fusion
  135.3 1.2 copy-done
  136.5 1.9 convolution_convert_fusion.2
  138.5 43.1 %all-gather.10.cloned.1.call-done = bf16[1088,1088]{0,1:T(8,128)(2,1)} async-done(((bf16[1088,136]{0,1:T(8,128)(2,1)}), bf16[1088,1088]{0,1:T(8,128)(2,1)}) %all-gather.10.cloned.1.call-update) | async-done | bytes 2367504 | tf_op jit(solution)/shard_map/all_gather | solution.py:118
  181.6 2.7 fusion.26
  184.5 1.2 add_convert_fusion
  185.7 134.3 %all-gather.14.cloned.1.call-done = bf16[4352,1088]{0,1:T(8,128)(2,1)} async-done(((bf16[4352,136]{0,1:T(8,128)(2,1)}), bf16[4352,1088]{0,1:T(8,128)(2,1)}) %all-gather.14.cloned.1.call-update) | async-done | bytes 9469968 | tf_op jit(solution)/shard_map/all_gather | solution.py:145
  320.0 8.4 fusion.27
  328.4 136.7 %all-gather.12.cloned.1.call-done = bf16[1088,4352]{0,1:T(8,128)(2,1)} async-done(((bf16[1088,544]{0,1:T(8,128)(2,1)}), bf16[1088,4352]{0,1:T(8,128)(2,1)}) %all-gather.12.cloned.1.call-update) | async-done | bytes 9469968 | tf_op jit(solution)/shard_map/all_gather | solution.py:144
  465.0 10.1 fusion.21
  475.1 4.1 copy.91
  479.3 4.4 convolution_bitcast_fusion
  483.7 7.1 copy.92
  490.9 9.4 multiply_reduce_fusion
  500.3 0.7 fusion.23
  501.1 1.5 copy-done.23
  502.6 1.2 convolution_convert_fusion
  504.6 1.6 multiply_convert_fusion
  506.2 0.8 convolution_convert_fusion.1
  507.6 1.2 fusion.24
  509.0 1.1 copy-done.15
  510.2 2.7 convolution_bitcast_fusion.2
  512.9 7.6 copy.86
  520.5 3.1 copy.89
  523.7 4.2 convolution_bitcast_fusion.1
  527.9 9.2 copy.90
  537.2 1.0 copy-done.18
  538.4 1.1 convolution_bitcast_fusion.3
  539.5 3.2 copy.87
  542.7 160.1 %reduce-scatter.15.cloned.1.call-done = f32[1,1088,136]{1,2,0:T(8,128)} async-done(((f32[32,1088,136]{1,2,0:T(8,128)}), f32[1,1088,136]{1,2,0:T(8,128)}) %reduce-scatter.15.cloned.1.call-update) | async-done | bytes 591888
  702.9 381.0 %reduce-scatter.9.cloned.1.call-done = f32[1,272,408]{2,1,0:T(8,128)} async-done(((f32[32,272,408]{2,1,0:T(8,128)}), f32[1,272,408]{2,1,0:T(8,128)}) %reduce-scatter.9.cloned.1.call-update) | async-done | bytes 443920 | tf_op jit(solution)/shard_map/reduce_scatter | solution.py:209
  1084.0 473.4 %reduce-scatter.11.cloned.1.call-done = f32[1,272,544]{2,1,0:T(8,128)} async-done(((f32[32,272,544]{2,1,0:T(8,128)}), f32[1,272,544]{2,1,0:T(8,128)}) %reduce-scatter.11.cloned.1.call-update) | async-done | bytes 591888 | tf_op jit(solution)/shard_map/reduce_scatter | solution.py:211
  1557.6 7.5 multiply_reduce_fusion.1
  1565.1 41.4 %all-reduce.11 = (f32[1088]{0:T(1024)S(1)}, f32[1088]{0:T(1024)S(1)}, f32[1088]{0:T(1024)S(1)}, f32[1088]{0:T(1024)S(1)}, f32[1088]{0:T(1024)S(1)}, /*index=5*/f...) all-reduce(f32[1088]{0:T(1024)S(1)} %get-tuple-element.117, ...), channel_id=1, replica_groups=mesh['rep'=4,'grp'=8] {'rep','grp'}, use_global_device_ids=true, to_apply=%region_14.15 | all-reduce | flops 13056 | bytes 104448 | tf_op jit(solution)/shard_map/psum | solution.py:221
  1606.5 0.6 dynamic_slice.27
  1607.1 0.6 dynamic_slice.28
  1607.8 0.6 dynamic_slice.29
  1608.4 0.6 dynamic_slice.30
  1609.1 0.6 dynamic_slice.31
  1609.7 0.6 dynamic_slice.32
  1610.3 0.6 dynamic_slice.33
  1611.0 0.6 dynamic_slice.35
  1611.6 0.7 dynamic_slice.34
  1612.3 2.7 multiply_add_fusion
  1615.0 7.4 fusion.11
  1622.4 58.7 %reduce-scatter.13.cloned.1.call-done = f32[1,272,136]{1,2,0:T(8,128)} async-done(((f32[32,272,136]{1,2,0:T(8,128)}), f32[1,272,136]{1,2,0:T(8,128)}) %reduce-scatter.13.cloned.1.call-update) | async-done | bytes 147984
  1681.1 9.2 all_gather.71
  1690.5 1.2 reshape.310
  1691.7 14.9 all-gather.20.cloned.1.call-done
  1706.6 3.8 copy.93
  1710.4 3.8 reshape.318
  1714.2 17.1 all-gather.16.cloned.1.call-done
  1731.3 2.9 copy.94
  1734.2 25.2 %all-gather.18.cloned.1.call-done = f32[4,272,544]{2,1,0:T(8,128)} async-done(((f32[1,272,544]{2,1,0:T(8,128)}), f32[4,272,544]{2,1,0:T(8,128)}) %all-gather.18.cloned.1.call-update) | async-done | bytes 2367504 | tf_op jit(solution)/shard_map/all_gather | solution.py:217
  1759.4 3.4 copy.95
  (140 shorter events, 8.1 us)
Async XLA Ops:
  7.2 3.0 copy-start.33
  7.2 4.9 copy-start.24
  7.2 5.6 copy-start.25
  7.2 5.9 copy-start.26
  7.2 6.1 copy-start.27
  7.2 6.3 copy-start.28
  7.2 6.6 copy-start.29
  7.3 6.8 copy-start.30
  7.3 7.1 copy-start.31
  7.3 7.3 copy-start.32
  7.3 7.6 copy-start.22
  7.3 50.1 %copy-start.1 = (f32[256,1088]{0,1:T(8,128)S(1)}, f32[256,1088]{0,1:T(8,128)}, u32[]{:S(2)}) copy-start(f32[256,1088]{0,1:T(8,128)} %param.24) | copy-start | bytes 3342340
  7.3 120.7 %all-gather.8.cloned.1.call-start = ((), (), s32[]{:S(2)}) async-start(), calls=%async_computation.4 | async-start | bytes 8460288 | tf_op jit(solution)/shard_map/all_gather | solution.py:117
  8.0 173.5 %all-gather.10.cloned.1.call-start = ((), (), s32[]{:S(2)}) async-start(), calls=%async_computation.5 | async-start | bytes 2820096 | tf_op jit(solution)/shard_map/all_gather | solution.py:118
  8.8 50.5 %copy-start.6 = (f32[256,1088]{0,1:T(8,128)S(1)}, f32[256,1088]{0,1:T(8,128)}, u32[]{:S(2)}) copy-start(f32[256,1088]{0,1:T(8,128)} %param.26) | copy-start | bytes 3342340
  8.8 311.2 %all-gather.14.cloned.1.call-start = ((), (), s32[]{:S(2)}) async-start(), calls=%async_computation.7 | async-start | bytes 10653696 | tf_op jit(solution)/shard_map/all_gather | solution.py:145
  9.5 455.5 %all-gather.12.cloned.1.call-start = ((), (), s32[]{:S(2)}) async-start(), calls=%async_computation.6 | async-start | bytes 11280384 | tf_op jit(solution)/shard_map/all_gather | solution.py:144
  10.1 692.7 %reduce-scatter.15.cloned.1.call-start = ((), (), s32[]{:S(2)}) async-start(), calls=%async_computation.14 | async-start | bytes 20680704
  59.8 73.7 %copy-start.14 = (bf16[256,1088]{0,1:T(8,128)(2,1)}, bf16[256,1088]{0,1:T(8,128)(2,1)S(1)}, u32[]{:S(2)}) copy-start(bf16[256,1088]{0,1:T(8,128)(2,1)S(1)} %add_convert_fusion.1) | copy-start | bytes 1671172
  133.5 1.9 copy-start.8
  134.4 2.2 copy-start
  184.3 316.0 %copy-start.2 = (f32[256,1088]{0,1:T(8,128)}, f32[256,1088]{0,1:T(8,128)S(1)}, u32[]{:S(2)}) copy-start(f32[256,1088]{0,1:T(8,128)S(1)} %get-tuple-element.154) | copy-start | bytes 3342340
  490.8 13.3 slice-start
  490.8 593.1 %reduce-scatter.9.cloned.1.call-start = ((), (), s32[]{:S(2)}) async-start(), calls=%async_computation.8 | async-start | bytes 18382848 | tf_op jit(solution)/shard_map/reduce_scatter | solution.py:209
  490.8 9.4 copy-start.7
  490.9 13.3 slice-start.1
  500.3 2.3 copy-start.23
  501.0 2.8 copy-start.4
  502.6 1.5 copy-start.19
  502.6 1.3 copy-start.17
  502.6 2.0 copy-start.9
  507.0 1.9 copy-start.10
  507.6 1.3 copy-start.12
  508.9 4.0 copy-start.21
  508.9 1.3 copy-start.15
  520.5 1036.9 %reduce-scatter.11.cloned.1.call-start = ((), (), s32[]{:S(2)}) async-start(), calls=%async_computation.10 | async-start | bytes 22978560 | tf_op jit(solution)/shard_map/reduce_scatter | solution.py:211
  537.1 1.1 copy-start.18
  537.1 1.3 copy-start.20
  537.2 1143.9 %reduce-scatter.13.cloned.1.call-start = ((), (), s32[]{:S(2)}) async-start(), calls=%async_computation.13 | async-start | bytes 6893568
  542.7 1014.9 %copy-start.11 = (bf16[17,64,256]{2,1,0:T(8,128)(2,1)S(1)}, bf16[17,64,256]{2,1,0:T(8,128)(2,1)}, u32[]{:S(2)}) copy-start(bf16[17,64,256]{2,1,0:T(8,128)(2,1)} %copy-done.10) | copy-start | bytes 1671172
  542.7 1014.9 %copy-start.13 = (bf16[256,17,64]{0,2,1:T(8,128)(2,1)S(1)}, bf16[256,17,64]{0,2,1:T(8,128)(2,1)}, u32[]{:S(2)}) copy-start(bf16[256,17,64]{0,2,1:T(8,128)(2,1)} %copy-done.12) | copy-start | bytes 1671172
  542.7 1163.9 %all-gather.20.cloned.1.call-start = ((), (), s32[]{:S(2)}) async-start(), calls=%async_computation.12 | async-start | bytes 3133440 | tf_op jit(solution)/shard_map/all_gather | solution.py:218
  702.9 1028.4 %all-gather.16.cloned.1.call-start = ((), (), s32[]{:S(2)}) async-start(), calls=%async_computation.9 | async-start | bytes 2785280 | tf_op jit(solution)/shard_map/all_gather | solution.py:215
  1083.9 675.4 %all-gather.18.cloned.1.call-start = ((), (), s32[]{:S(2)}) async-start(), calls=%async_computation.11 | async-start | bytes 3481600 | tf_op jit(solution)/shard_map/all_gather | solution.py:217
  1557.6 54.7 %copy-start.5 = (f32[256,1088]{0,1:T(8,128)S(1)}, f32[256,1088]{0,1:T(8,128)}, u32[]{:S(2)}) copy-start(f32[256,1088]{0,1:T(8,128)} %copy-done.4) | copy-start | bytes 3342340
  1612.3 2.7 copy-start.3
  1612.3 2.7 copy-start.16
Sparse Core Ops, SparseCore 0:
  10.3 117.6 all-gather.7
  130.2 51.3 all-gather.9
  183.8 136.1 all-gather.13
  322.0 142.9 all-gather.11
  490.9 211.9 reduce-scatter.14
  705.0 378.8 reduce-scatter.8
  1086.2 471.1 reduce-scatter.10
  1563.1 117.9 reduce-scatter.12
  1682.6 23.8 all-gather.19
  1708.0 23.2 all-gather.15
  1732.9 26.4 all-gather.17
where the time goes:
time: 1770 us
  waiting for transfers between devices  1520 us (86%)
  blocking collectives  92.8 us (5%)
  matrix products  71.6 us (4%)
  local copies, waits for them, and re-layouts  64.8 us (4%)
    reduce_scatter x1, waiting for transfers between devices, per_device(): lax.psum_scatter(blocks[2], ('rep', 'grp'), scatter_dimension=0, tiled=True)  473 us
    reduce_scatter x1, waiting for transfers between devices, per_device(): lax.psum_scatter(blocks[0], ('rep', 'grp'), scatter_dimension=0, tiled=True)  381 us
    unnamed x13, waiting for transfers between devices  221 us
    all_gather x1, waiting for transfers between devices, per_device(): lax.all_gather(expand_weight, 'grp', axis=1, tiled=True)  137 us
    all_gather x1, waiting for transfers between devices, per_device(): lax.all_gather(contract_weight, 'grp', axis=1, tiled=True)  134 us
    all_gather x1, waiting for transfers between devices, per_device(): lax.all_gather(attention_in, 'grp', axis=1, tiled=True)  68.2 us
    dot_general x8, matrix products, matmul(): return jnp.dot(left, right, preferred_element_type=jnp.float32)  52.2 us
    all_gather x1, waiting for transfers between devices, per_device(): lax.all_gather(attention_out, 'grp', axis=1, tiled=True)  43.1 us
  transfers between devices with their start and end apart: 11, of which 11 were waited for; matrix products, arithmetic and copies ran while one was open for 6% of the time, Pallas kernels for 0%

commit v1 on v0

v1 whole, which is shorter than its diff:
```python
import functools

import jax
import jax.numpy as jnp
from jax import lax
from jax.experimental import pallas as pl
from jax.experimental.pallas import tpu as pltpu
from jax.sharding import PartitionSpec as P

HD = 64
EPSILON = 1e-05
MASKED = -1e30
YSIZE = 2
MESH_ID = pl.DeviceIdType.MESH
VMEM_LIMIT = 67043328


def layer_norm(values, gain, shift):
    center = values - jnp.mean(values, axis=-1, keepdims=True)
    inverse = lax.rsqrt(jnp.mean(center * center, axis=-1, keepdims=True) + EPSILON)
    normed = center * inverse
    return (normed, inverse, normed * gain.astype(jnp.float32) + shift.astype(jnp.float32))


def norm_back(upstream, normed, inverse, gain):
    scaled = upstream * gain.astype(jnp.float32)
    return inverse * (
        scaled
        - jnp.mean(scaled, axis=-1, keepdims=True)
        - normed * jnp.mean(scaled * normed, axis=-1, keepdims=True)
    )


def product(form, left, right):
    return jnp.einsum(form, left, right, preferred_element_type=jnp.float32)


def document_layout(lengths, count):
    ends = jnp.cumsum(lengths)
    slots = jnp.arange(count, dtype=jnp.int32)
    number = jnp.sum((slots[:, None] >= ends[None, :]).astype(jnp.int32), axis=1)
    valid = slots < ends[-1]
    labels = jnp.where(valid, number, lengths.shape[0] + slots)
    return (valid, labels)


class Place:
    def __init__(self, rep_count, grp_count):
        self.R, self.G = rep_count, grp_count
        self.Y = YSIZE
        self.Z = grp_count // YSIZE
        self.r = lax.axis_index("rep")
        self.g = lax.axis_index("grp")
        self.c = self.r % 2
        self.m = self.r // 2
        self.xi = self.m % 2
        self.z = self.g // YSIZE
        self.y = self.g % YSIZE
        self.partner = (self.r + 1 - 2 * self.c, self.g)
        self.xnbr = (self.r + 2 - 4 * self.xi, self.g)
        self.ynbr = (self.r, self.g + 1 - 2 * self.y)
        self.up = (self.r, self.g + YSIZE)
        self.down = (self.r, self.g - YSIZE)

    def flip_rep(self, bit):
        on = (self.r // (1 << bit)) % 2
        return (self.r + (1 << bit) - (2 << bit) * on, self.g)

    def flip_grp(self, bit):
        on = (self.g // (1 << bit)) % 2
        return (self.r, self.g + (1 << bit) - (2 << bit) * on)


def greet(here, others):
    barrier = pltpu.get_barrier_semaphore()

    def hello(target):
        pl.semaphore_signal(barrier, inc=1, device_id=target, device_id_type=MESH_ID)

    for target in [here.partner, here.xnbr, here.ynbr] + others:
        hello(target)

    @pl.when(here.z < here.Z - 1)
    def _():
        hello(here.up)

    @pl.when(here.z > 0)
    def _():
        hello(here.down)

    inner = jnp.where((here.z > 0) & (here.z < here.Z - 1), 1, 0)
    pl.semaphore_wait(barrier, 4 + len(others) + inner)


def remote(src, dst, send, recv, target):
    return pltpu.make_async_remote_copy(
        src_ref=src, dst_ref=dst, send_sem=send, recv_sem=recv, device_id=target, device_id_type=MESH_ID
    )


def bits_of(count):
    return count.bit_length() - 1


def gather_kernel(
    R,
    G,
    share,
    ahead,
    own_ref,
    small_ref,
    all_ref,
    small_all,
    bounce,
    local_sem,
    small_send,
    small_recv,
    send_own,
    send_fwd,
    send_y,
    send_x,
    send_cp,
    send_cx,
    recv_p,
    recv_x,
    recv_cp,
    recv_cx,
):
    here = Place(R, G)
    N, n = own_ref.shape[0], own_ref.shape[1]
    Z = here.Z
    y, z, c, xi = here.y, here.z, here.c, here.xi
    width = n - share
    start = pl.multiple_of(xi * share, 8)
    give = pl.multiple_of(xi * width, 8)
    take = pl.multiple_of((1 - xi) * width, 8)
    grp_bits = bits_of(G)
    extra = [here.flip_grp(b) for b in range(2, grp_bits)]
    greet(here, extra)

    pull = pltpu.make_async_copy(own_ref, bounce, local_sem.at[0])
    pull.start()

    def plane(k, g):
        return all_ref.at[g, k, pl.ds(start, width), :]

    def gift(k, g):
        return all_ref.at[g, k, pl.ds(give, share), :]

    def due(k, g):
        return all_ref.at[g, k, pl.ds(take, share), :]

    def own_part(k):
        return own_ref.at[k, pl.ds(start, width), :]

    def shard(zz, yy):
        return zz * YSIZE + yy

    def own_copy(k, way):
        target = (here.up, here.down, here.ynbr)[way]
        return remote(own_part(k), plane(k, here.g), send_own.at[k, way], recv_p.at[k, z], target)

    def passing(k, zz):
        step = jnp.where(zz < z, YSIZE, -YSIZE)
        ref = plane(k, shard(zz, y))
        return remote(ref, ref, send_fwd.at[k, zz], recv_p.at[k, zz], (here.r, here.g + step))

    def over_y(k, zz):
        ref = plane(k, shard(zz, y))
        return remote(ref, ref, send_y.at[k, zz], recv_p.at[k, zz], here.ynbr)

    def over_x(k, zz):
        ref = gift(k, shard(zz, c))
        return remote(ref, ref, send_x.at[k, zz], recv_x.at[k, zz], here.xnbr)

    def plane_to_partner(k, zz):
        ref = plane(k, shard(zz, c))
        return remote(ref, ref, send_cp.at[k, zz], recv_cp.at[k, zz], here.partner)

    def rest_to_partner(k, zz):
        ref = due(k, shard(zz, c))
        return remote(ref, ref, send_cx.at[k, zz], recv_cx.at[k, zz], here.partner)

    def from_partner_plane(k, zz):
        ref = plane(k, shard(zz, 1 - c))
        return remote(ref, ref, send_cp.at[k, zz], recv_cp.at[k, zz], here.partner)

    def from_partner_rest(k, zz):
        ref = due(k, shard(zz, 1 - c))
        return remote(ref, ref, send_cx.at[k, zz], recv_cx.at[k, zz], here.partner)

    def x_arrival(k, zz):
        ref = due(k, shard(zz, c))
        return remote(ref, ref, send_x.at[k, zz], recv_x.at[k, zz], here.xnbr)

    def nth(i):
        table = [sorted([q for q in range(Z) if q != p], key=lambda q: abs(q - p)) for p in range(Z)]
        pick = table[0][i]
        for p in range(1, Z):
            pick = jnp.where(z == p, table[p][i], pick)
        return pick

    def goes_on(zz):
        return ((zz < z) & (z < Z - 1)) | ((zz > z) & (z > 0))

    source = y == c

    def small_copy(bit):
        size = 1 << bit
        base = (here.g // size) * size
        ref = small_all.at[pl.ds(base, size)]
        return remote(ref, ref, small_send.at[bit], small_recv.at[bit], here.flip_grp(bit))

    def small_arrival(bit):
        size = 1 << bit
        base = (here.g // size) * size
        base = base + size - 2 * size * ((here.g // size) % 2)
        ref = small_all.at[pl.ds(base, size)]
        return remote(ref, ref, small_send.at[bit], small_recv.at[bit], here.flip_grp(bit))

    def body(t, carry):
        @pl.when((t < N) & source)
        def _():
            @pl.when(z < Z - 1)
            def _():
                own_copy(t, 0).start()

            @pl.when(z > 0)
            def _():
                own_copy(t, 1).start()

            own_copy(t, 2).start()

        k = t - ahead

        @pl.when((k >= 0) & (k < N) & source)
        def _():
            def arrival(i, carry):
                zz = nth_dynamic(i)
                passing(k, zz).wait_recv()

                @pl.when(goes_on(zz))
                def _():
                    passing(k, zz).start()

                over_y(k, zz).start()
                over_x(k, zz).start()
                plane_to_partner(k, zz).start()
                return carry

            lax.fori_loop(0, Z - 1, arrival, 0)

        @pl.when((k >= 0) & (k < N) & (y != c))
        def _():
            def arrival(i, carry):
                zz = jnp.where(i == 0, z, nth_dynamic(i - 1))
                ref = plane(k, shard(zz, c))
                remote(ref, ref, send_y.at[k, zz], recv_p.at[k, zz], here.ynbr).wait_recv()
                over_x(k, zz).start()
                plane_to_partner(k, zz).start()
                return carry

            lax.fori_loop(0, Z, arrival, 0)

        q = t - ahead - 1

        @pl.when((q >= 0) & (q < N))
        def _():
            def arrival(zz, carry):
                @pl.when((y != c) | (zz != z))
                def _():
                    x_arrival(q, zz).wait_recv()
                    rest_to_partner(q, zz).start()

                return carry

            lax.fori_loop(0, Z, arrival, 0)

        return carry

    def nth_dynamic(i):
        pick = nth(0)
        for j in range(1, Z - 1):
            pick = jnp.where(i == j, nth(j), pick)
        return pick

    seed = pltpu.make_async_copy(small_ref, small_all.at[here.g], local_sem.at[1])
    seed.start()
    seed.wait()
    for bit in range(grp_bits):
        small_copy(bit).start()
        if bit == 0:
            lax.fori_loop(0, ahead, body, 0)
        small_arrival(bit).wait_recv()
    pull.wait()
    push = pltpu.make_async_copy(bounce, all_ref.at[here.g], local_sem.at[0])
    push.start()
    lax.fori_loop(ahead, N + ahead + 1, body, 0)
    push.wait()

    def settle(k, carry):
        @pl.when(source)
        def _():
            @pl.when(z < Z - 1)
            def _():
                own_copy(k, 0).wait_send()

            @pl.when(z > 0)
            def _():
                own_copy(k, 1).wait_send()

            own_copy(k, 2).wait_send()

        def each(zz, carry):
            @pl.when((y != c) | (zz != z))
            def _():
                over_x(k, zz).wait_send()
                plane_to_partner(k, zz).wait_send()
                rest_to_partner(k, zz).wait_send()

            @pl.when(source & (zz != z))
            def _():
                over_y(k, zz).wait_send()

                @pl.when(goes_on(zz))
                def _():
                    passing(k, zz).wait_send()

            @pl.when((y == c) | (zz != z))
            def _():
                from_partner_plane(k, zz).wait_recv()
                from_partner_rest(k, zz).wait_recv()

            return carry

        lax.fori_loop(0, Z, each, 0)
        return carry

    lax.fori_loop(0, N, settle, 0)
    for bit in range(grp_bits):
        small_copy(bit).wait_send()


def gather_all(own, small, R, G):
    N, n, K = own.shape
    Z = G // YSIZE
    bits = bits_of(G)
    share = (6 * n // 17) // 8 * 8
    dma = pltpu.SemaphoreType.DMA
    return pl.pallas_call(
        functools.partial(gather_kernel, R, G, share, 2),
        out_shape=(
            jax.ShapeDtypeStruct((G, N, n, K), jnp.bfloat16),
            jax.ShapeDtypeStruct((G,) + small.shape, jnp.bfloat16),
        ),
        in_specs=[pl.BlockSpec(memory_space=pl.ANY)] * 2,
        out_specs=(pl.BlockSpec(memory_space=pl.ANY),) * 2,
        scratch_shapes=[
            pltpu.VMEM((N, n, K), jnp.bfloat16),
            dma((2,)),
            dma((bits,)),
            dma((bits,)),
            dma((N, 3)),
        ]
        + [dma((N, Z))] * 9,
        compiler_params=pltpu.CompilerParams(collective_id=0, has_side_effects=True, vmem_limit_bytes=VMEM_LIMIT),
        name="gather_all",
    )(own, small)


def reduce_kernel(
    R,
    G,
    share,
    con_count,
    exp_count,
    dy_ref,
    x_ref,
    vec_ref,
    out_ref,
    vec_out,
    pair_buf,
    dyo,
    dyp,
    xo,
    xp,
    plane,
    xs,
    xb,
    yb,
    zb,
    fx,
    fin,
    pair_tmp,
    vec_buf,
    vec_got,
    dy_local,
    x_local,
    dy_send,
    dy_recv,
    x_send,
    x_recv,
    xs_send,
    xs_recv,
    y_send,
    y_recv,
    z_send,
    z_recv,
    f_send,
    f_recv,
    o_local,
    o_send,
    o_recv,
    pair_send,
    pair_recv,
    pair_local,
    vec_send,
    vec_recv,
):
    here = Place(R, G)
    Z = here.Z
    y, z, c, xi = here.y, here.z, here.c, here.xi
    N, n = out_ref.shape[0], out_ref.shape[1]
    D_N, X_N = dy_ref.shape[0], x_ref.shape[0]
    width = n - share
    rep_bits, grp_bits = bits_of(R), bits_of(G)
    rounds = rep_bits + grp_bits
    extra = [here.flip_grp(b) for b in range(2, grp_bits)] + [here.flip_rep(b) for b in range(2, rep_bits)]
    greet(here, extra)
    sink = y == c

    def dy_local_copy(i):
        return pltpu.make_async_copy(dy_ref.at[i, :, c], dyo.at[i], dy_local.at[i])

    def x_local_copy(i):
        return pltpu.make_async_copy(x_ref.at[i], xo.at[i], x_local.at[i])

    def dy_swap(i):
        return remote(dy_ref.at[i, :, 1 - c], dyp.at[i], dy_send.at[i], dy_recv.at[i], here.partner)

    def x_swap(i):
        return remote(x_ref.at[i], xp.at[i], x_send.at[i], x_recv.at[i], here.partner)

    order = [("d", 0)] + [("x", i) for i in range(con_count)]
    order += [("d", 1), ("x", con_count)] + [("d", i) for i in range(2, 1 + exp_count)]
    order += [("d", 1 + exp_count), ("x", con_count + 1), ("d", 2 + exp_count), ("x", con_count + 2)]
    order += [("d", i) for i in range(3 + exp_count, D_N)]
    for kind, i in order:
        if kind == "d":
            dy_swap(i).start()
            dy_local_copy(i).start()
        else:
            x_swap(i).start()
            x_local_copy(i).start()

    def dy_of(k):
        return jnp.maximum(k - (con_count - 1), 0)

    def x_of(k):
        first, second = con_count + exp_count, con_count + exp_count + 1
        return jnp.where(
            k < con_count, k, jnp.where(k < first, con_count, jnp.where(k < second, con_count + 1, con_count + 2))
        )

    def x_copy(k, zz):
        return remote(xs.at[k, zz], xb.at[k, zz], xs_send.at[k, zz], xs_recv.at[k, zz], here.xnbr)

    def y_copy(k, zz):
        return remote(plane.at[k, zz], yb.at[k, zz], y_send.at[k, zz], y_recv.at[k, zz], here.ynbr)

    def up_copy(k, zz):
        return remote(plane.at[k, zz], zb.at[k, zz], z_send.at[k, zz], z_recv.at[k, zz], here.up)

    def down_slot(zz, at):
        return jnp.where(zz == at, Z, zz)

    def down_copy(k, zz):
        slot = down_slot(zz, z - 1)
        return remote(plane.at[k, zz], zb.at[k, slot], z_send.at[k, zz], z_recv.at[k, slot], here.down)

    def z_arrival(k, slot, target):
        return remote(plane.at[k, 0], zb.at[k, slot], z_send.at[k, 0], z_recv.at[k, slot], target)

    def f_copy(k):
        return remote(plane.at[k, z], fx.at[k], f_send.at[k], f_recv.at[k], here.xnbr)

    def o_keep(k):
        return pltpu.make_async_copy(fin.at[k % 2], out_ref.at[k], o_local.at[k])

    def o_give(k):
        return remote(fin.at[k % 2], out_ref.at[k], o_send.at[k], o_recv.at[k], here.partner)

    def f32(value):
        return value.astype(jnp.float32)

    def multiply(k):
        di, xj = dy_of(k), x_of(k)

        @pl.when((k == 0) | (k >= con_count))
        def _():
            dy_local_copy(di).wait()
            dy_swap(di).wait_recv()

        @pl.when((k <= con_count) | (k == con_count + exp_count) | (k == con_count + exp_count + 1))
        def _():
            x_local_copy(xj).wait()
            x_swap(xj).wait_recv()

        def each(zz, carry):
            term = jnp.dot(dyo[di, zz], xo[xj], preferred_element_type=jnp.float32)
            term = term + jnp.dot(dyp[di, zz], xp[xj], preferred_element_type=jnp.float32)

            @pl.when(xi == 0)
            def _():
                plane[k, zz] = term[:width].astype(jnp.bfloat16)
                xs[k, zz] = term[width:].astype(jnp.bfloat16)

            @pl.when(xi == 1)
            def _():
                plane[k, zz] = term[share:].astype(jnp.bfloat16)
                xs[k, zz] = term[:share].astype(jnp.bfloat16)

            x_copy(k, zz).start()
            return carry

        lax.fori_loop(0, Z, each, 0)

    def after_x(k):
        def each(zz, carry):
            x_copy(k, zz).wait_recv()
            got = f32(xb[k, zz])

            @pl.when(xi == 0)
            def _():
                plane[k, zz, :share] = (f32(plane[k, zz, :share]) + got).astype(jnp.bfloat16)

            @pl.when(xi == 1)
            def _():
                low = width - share
                plane[k, zz, low:] = (f32(plane[k, zz, low:]) + got).astype(jnp.bfloat16)

            @pl.when(y != c)
            def _():
                y_copy(k, zz).start()

            return carry

        lax.fori_loop(0, Z, each, 0)

    def after_y(k):
        @pl.when(sink)
        def _():
            def each(zz, carry):
                y_copy(k, zz).wait_recv()
                plane[k, zz] = (f32(plane[k, zz]) + f32(yb[k, zz])).astype(jnp.bfloat16)
                return carry

            lax.fori_loop(0, Z, each, 0)

            def line(i, carry):
                high = Z - 1 - i

                @pl.when(high > z)
                def _():
                    @pl.when(z > 0)
                    def _():
                        z_arrival(k, high, here.down).wait_recv()
                        plane[k, high] = (f32(plane[k, high]) + f32(zb[k, high])).astype(jnp.bfloat16)

                    up_copy(k, high).start()

                @pl.when(i < z)
                def _():
                    @pl.when(z < Z - 1)
                    def _():
                        z_arrival(k, i, here.up).wait_recv()
                        plane[k, i] = (f32(plane[k, i]) + f32(zb[k, i])).astype(jnp.bfloat16)

                    down_copy(k, i).start()

                return carry

            lax.fori_loop(0, Z - 1, line, 0)

    def after_z(k):
        @pl.when(sink)
        def _():
            @pl.when(z == 0)
            def _():
                z_arrival(k, Z, here.up).wait_recv()
                plane[k, z] = (f32(plane[k, z]) + f32(zb[k, Z])).astype(jnp.bfloat16)

            @pl.when(z == Z - 1)
            def _():
                z_arrival(k, z, here.down).wait_recv()
                plane[k, z] = (f32(plane[k, z]) + f32(zb[k, z])).astype(jnp.bfloat16)

            @pl.when((z > 0) & (z < Z - 1))
            def _():
                z_arrival(k, z, here.down).wait_recv()
                z_arrival(k, Z, here.up).wait_recv()
                plane[k, z] = (f32(plane[k, z]) + f32(zb[k, z]) + f32(zb[k, Z])).astype(jnp.bfloat16)

            f_copy(k).start()

    def finish(k):
        @pl.when(sink)
        def _():
            f_copy(k).wait_recv()

            @pl.when(k >= 2)
            def _():
                o_keep(k - 2).wait()
                o_give(k - 2).wait_send()

            slot = k % 2

            def assemble(first, second):
                fin[slot, :share] = f32(first[:share])
                fin[slot, share:width] = f32(first[share:]) + f32(second[: width - share])
                fin[slot, width:] = f32(second[width - share :])

            @pl.when(xi == 0)
            def _():
                assemble(plane[k, z], fx[k])

            @pl.when(xi == 1)
            def _():
                assemble(fx[k], plane[k, z])

            for bit in range(2, rep_bits):
                j = bit - 2
                give = remote(fin.at[slot], pair_buf.at[k, j], pair_send, pair_recv.at[k, j], here.flip_rep(bit))
                give.start()
                give.wait()
                bring = pltpu.make_async_copy(pair_buf.at[k, j], pair_tmp, pair_local)
                bring.start()
                bring.wait()
                fin[slot] = fin[slot] + pair_tmp[...]
            o_keep(k).start()
            o_give(k).start()

    def vec_copy(i):
        target_r, target_g = here.flip_rep(0)
        for b in range(1, rep_bits):
            other = here.flip_rep(b)
            target_r = jnp.where(i == b, other[0], target_r)
            target_g = jnp.where(i == b, other[1], target_g)
        for b in range(grp_bits):
            other = here.flip_grp(b)
            target_r = jnp.where(i == rep_bits + b, other[0], target_r)
            target_g = jnp.where(i == rep_bits + b, other[1], target_g)
        return remote(vec_buf.at[i], vec_got.at[i], vec_send.at[i], vec_recv.at[i], (target_r, target_g))

    vec_buf[0] = vec_ref[...]
    vec_copy(0).start()

    def body(t, carry):
        @pl.when(t < N)
        def _():
            multiply(t)

        @pl.when((t >= 1) & (t < N + 1))
        def _():
            after_x(t - 1)

        @pl.when((t >= 2) & (t < N + 2))
        def _():
            after_y(t - 2)

        @pl.when((t >= 3) & (t < N + 3))
        def _():
            after_z(t - 3)

        @pl.when((t >= 4) & (t < N + 4))
        def _():
            finish(t - 4)

        @pl.when(t < rounds)
        def _():
            vec_copy(t).wait_recv()
            vec_buf[t + 1] = vec_buf[t] + vec_got[t]

            @pl.when(t + 1 < rounds)
            def _():
                vec_copy(t + 1).start()

        return carry

    lax.fori_loop(0, N + 4, body, 0)
    vec_out[...] = vec_buf[rounds]

    def settle(k, carry):
        def each(zz, carry):
            x_copy(k, zz).wait_send()

            @pl.when(y != c)
            def _():
                y_copy(k, zz).wait_send()

            @pl.when(sink & (zz > z))
            def _():
                up_copy(k, zz).wait_send()

            @pl.when(sink & (zz < z))
            def _():
                down_copy(k, zz).wait_send()

            return carry

        lax.fori_loop(0, Z, each, 0)

        @pl.when(sink)
        def _():
            f_copy(k).wait_send()

            @pl.when(k >= N - 2)
            def _():
                o_keep(k).wait()
                o_give(k).wait_send()

        @pl.when(y != c)
        def _():
            o_give(k).wait_recv()

        return carry

    lax.fori_loop(0, N, settle, 0)
    for i in range(D_N):
        dy_swap(i).wait_send()
    for i in range(X_N):
        x_swap(i).wait_send()
    for i in range(rounds):
        vec_copy(i).wait_send()


def reduce_all(dy, xs, vec, con_count, exp_count, N, R, G):
    D_N, _, _, n, T = dy.shape
    X_N, _, K = xs.shape
    Z = G // YSIZE
    share = (5 * n // 17) // 8 * 8
    width = n - share
    dma = pltpu.SemaphoreType.DMA
    rounds = bits_of(R) + bits_of(G)
    pairs = max(bits_of(R) - 2, 1)
    deep = bits_of(R) > 2
    bf16, f32 = jnp.bfloat16, jnp.float32
    hbm = pl.BlockSpec(memory_space=pl.ANY)
    vmem = pl.BlockSpec(memory_space=pltpu.VMEM)
    out, vec_sum, _ = pl.pallas_call(
        functools.partial(reduce_kernel, R, G, share, con_count, exp_count),
        out_shape=(
            jax.ShapeDtypeStruct((N, n, K), f32),
            jax.ShapeDtypeStruct(vec.shape, f32),
            jax.ShapeDtypeStruct((N, pairs, n, K) if deep else (1, 1, 8, 128), f32),
        ),
        in_specs=[hbm, hbm, vmem],
        out_specs=(hbm, vmem, hbm),
        scratch_shapes=[
            pltpu.VMEM((D_N, Z, n, T), bf16),
            pltpu.VMEM((D_N, Z, n, T), bf16),
            pltpu.VMEM((X_N, T, K), bf16),
            pltpu.VMEM((X_N, T, K), bf16),
            pltpu.VMEM((N, Z, width, K), bf16),
            pltpu.VMEM((N, Z, share, K), bf16),
            pltpu.VMEM((N, Z, share, K), bf16),
            pltpu.VMEM((N, Z, width, K), bf16),
            pltpu.VMEM((N, Z + 1, width, K), bf16),
            pltpu.VMEM((N, width, K), bf16),
            pltpu.VMEM((2, n, K), f32),
            pltpu.VMEM((n, K) if deep else (8, 128), f32),
            pltpu.VMEM((rounds + 1,) + vec.shape, f32),
            pltpu.VMEM((rounds,) + vec.shape, f32),
            dma((D_N,)),
            dma((X_N,)),
            dma((D_N,)),
            dma((D_N,)),
            dma((X_N,)),
            dma((X_N,)),
            dma((N, Z)),
            dma((N, Z)),
            dma((N, Z)),
            dma((N, Z)),
            dma((N, Z)),
            dma((N, Z + 1)),
            dma((N,)),
            dma((N,)),
            dma((N,)),
            dma((N,)),
            dma((N,)),
            dma,
            dma((N, pairs)),
            dma,
            dma((rounds,)),
            dma((rounds,)),
        ],
        compiler_params=pltpu.CompilerParams(collective_id=1, has_side_effects=True, vmem_limit_bytes=VMEM_LIMIT),
        name="reduce_all",
    )(dy, xs, vec)
    return out, vec_sum


def dot_nt(left, right):
    return lax.dot_general(left, right, (((1,), (1,)), ((), ())), preferred_element_type=jnp.float32)


def per_device(
    tokens,
    document_lengths,
    cotangent,
    first_gain,
    first_shift,
    attention_in,
    query_bias,
    value_bias,
    attention_out,
    output_bias,
    second_gain,
    second_shift,
    expand_weight,
    expand_bias,
    contract_weight,
    contract_bias,
):
    R, G = lax.axis_size("rep"), lax.axis_size("grp")
    T, D = tokens.shape
    H = D // HD
    n = D // G
    FF = contract_weight.shape[0]
    Q = FF // D
    bf16, f32 = jnp.bfloat16, jnp.float32
    valid, labels = document_layout(document_lengths[0], T)

    own = jnp.concatenate(
        [
            attention_in.T.reshape(3, n, D),
            attention_out.T.reshape(1, n, D),
            expand_weight.T.reshape(Q, n, D),
            jnp.swapaxes(contract_weight.reshape(Q, D, n), 1, 2),
        ],
        axis=0,
    )
    N = own.shape[0]
    parts = [
        first_gain,
        first_shift,
        query_bias,
        value_bias,
        output_bias,
        second_gain,
        second_shift,
        contract_bias,
        expand_bias,
    ]
    flat = jnp.concatenate(parts)
    rows = -(-flat.shape[0] // (8 * 128)) * 8
    small = jnp.pad(flat, (0, rows * 128 - flat.shape[0])).reshape(rows, 128)
    gathered, small_all = gather_all(own, small, R, G)
    small_all = small_all.reshape(G, rows * 128)
    full = []
    at = 0
    for part in parts:
        full.append(small_all[:, at : at + part.shape[0]].reshape(-1).astype(f32))
        at += part.shape[0]
    gain_one, shift_one, bias_query, bias_value, bias_output, gain_two, shift_two, bias_contract, bias_expand = full
    in_t = gathered[:, 0:3].reshape(3 * D, D)
    out_t = gathered[:, 3].reshape(D, D)
    exp_t = gathered[:, 4 : 4 + Q].reshape(Q, D, D)
    con_t = jnp.swapaxes(gathered[:, 4 + Q :], 0, 1).reshape(Q, D, D)

    normed_one, inverse_one, hidden_one = layer_norm(tokens, gain_one, shift_one)
    hidden_one = hidden_one.astype(bf16)
    bias_all = jnp.concatenate([bias_query, jnp.zeros((D,), f32), bias_value])
    projected = (dot_nt(hidden_one, in_t) + bias_all).astype(bf16)
    heads = projected.reshape(T, 3, H, HD)
    query, keyset, valueset = heads[:, 0], heads[:, 1], heads[:, 2]
    positions = jnp.arange(T, dtype=jnp.int32)
    allowed = (positions[None, :] <= positions[:, None]) & (labels[None, :] == labels[:, None])
    raw = product("qhd,khd->hqk", query, keyset) * HD ** (-0.5)
    scores = jnp.where(allowed[None], raw, MASKED)
    peak = jnp.max(scores, axis=-1, keepdims=True)
    logsum = peak + jnp.log(jnp.sum(jnp.exp(scores - peak), axis=-1, keepdims=True))
    probability = jnp.exp(scores - logsum)
    weights = probability.astype(bf16)
    attended = product("hqk,khd->qhd", weights, valueset).astype(bf16)
    flat_attended = attended.reshape(T, D)
    residual = tokens + dot_nt(flat_attended, out_t) + bias_output
    normed_two, inverse_two, hidden_two = layer_norm(residual, gain_two, shift_two)
    hidden_two = hidden_two.astype(bf16)
    before = product("tk,qnk->qtn", hidden_two, exp_t) + bias_expand.reshape(Q, 1, D)
    activated = jax.nn.gelu(before).astype(bf16)
    output = residual + product("qtk,qnk->tn", activated, con_t) + bias_contract
    live = valid[:, None]
    block_output = jnp.where(live, output, 0.0)
    start = jnp.where(live, cotangent, 0.0)
    start_low = start.astype(bf16)
    _, gelu_back = jax.vjp(jax.nn.gelu, before)
    back_before = gelu_back(product("tn,qnk->qtk", start_low, con_t))[0]
    back_before_low = back_before.astype(bf16)
    back_hidden_two = product("qtn,qnk->tk", back_before_low, exp_t)
    back_residual = start + norm_back(back_hidden_two, normed_two, inverse_two, gain_two)
    back_residual_low = back_residual.astype(bf16)
    back_attended = product("tn,nk->tk", back_residual_low, out_t).astype(bf16).reshape(T, H, HD)
    delta = jnp.sum(back_attended.astype(f32) * attended.astype(f32), axis=-1).T
    flow = product("qhd,khd->hqk", back_attended, valueset)
    slope = (probability * (flow - delta[:, :, None]) * HD ** (-0.5)).astype(bf16)
    back_query = product("hqk,khd->qhd", slope, keyset).reshape(T, D)
    back_key = product("hqk,qhd->khd", slope, query).reshape(T, D)
    back_value = product("hqk,qhd->khd", weights, back_attended).reshape(T, D)
    back_projected = jnp.concatenate([back_query, back_key, back_value], axis=1)
    back_projected_low = back_projected.astype(bf16)
    back_hidden_one = product("tn,nk->tk", back_projected_low, in_t)
    tokens_gradient = back_residual + norm_back(back_hidden_one, normed_one, inverse_one, gain_one)
    vectors = (
        jnp.sum(back_hidden_one * normed_one, axis=0),
        jnp.sum(back_hidden_one, axis=0),
        jnp.sum(back_query, axis=0),
        jnp.sum(back_value, axis=0),
        jnp.sum(back_residual, axis=0),
        jnp.sum(back_hidden_two * normed_two, axis=0),
        jnp.sum(back_hidden_two, axis=0),
        jnp.sum(start, axis=0),
        jnp.sum(back_before, axis=1).reshape(-1),
    )
    Z = G // YSIZE
    before_t = back_before_low.transpose(0, 2, 1).reshape(G, Q, n, T).transpose(1, 0, 2, 3)
    dy = jnp.concatenate(
        [
            start_low.T.reshape(1, G, n, T),
            before_t,
            back_residual_low.T.reshape(1, G, n, T),
            back_projected_low.T.reshape(G, 3, n, T).transpose(1, 0, 2, 3),
        ],
        axis=0,
    ).reshape(-1, Z, YSIZE, n, T)
    xs = jnp.concatenate([activated, hidden_two[None], flat_attended[None], hidden_one[None]], axis=0)
    flat_vec = jnp.concatenate(vectors)
    vec_rows = -(-flat_vec.shape[0] // (8 * 128)) * 8
    vec = jnp.pad(flat_vec, (0, vec_rows * 128 - flat_vec.shape[0])).reshape(vec_rows, 128)
    grads, vec_sum = reduce_all(dy, xs, vec, Q, Q, N, R, G)
    vec_sum = vec_sum.reshape(-1)
    place = lax.axis_index("grp")
    shares = []
    at = 0
    for vector in vectors:
        size = vector.shape[0]
        shares.append(lax.dynamic_slice_in_dim(vec_sum, at + place * (size // G), size // G))
        at += size
    con_grad = jnp.swapaxes(grads[0:Q], 1, 2).reshape(FF, n)
    exp_grad = grads[Q : 2 * Q].reshape(Q * n, D).T
    out_grad = grads[2 * Q].T
    in_grad = grads[2 * Q + 1 :].reshape(3 * n, D).T
    return (
        block_output,
        tokens_gradient,
        shares[0],
        shares[1],
        in_grad,
        shares[2],
        shares[3],
        out_grad,
        shares[4],
        shares[5],
        shares[6],
        exp_grad,
        shares[8],
        con_grad,
        shares[7],
    )


def solution(mesh):
    rows = P(("rep", "grp"), None)
    split, columns = P("grp"), P(None, "grp")
    return jax.shard_map(
        per_device,
        mesh=mesh,
        in_specs=(
            rows,
            rows,
            rows,
            split,
            split,
            columns,
            split,
            split,
            columns,
            split,
            split,
            split,
            columns,
            split,
            columns,
            split,
        ),
        out_specs=(
            rows,
            rows,
            split,
            split,
            columns,
            split,
            split,
            columns,
            split,
            split,
            split,
            columns,
            split,
            columns,
            split,
        ),
        check_vma=False,
    )
```

time: 1770 us -> 547 us (0.31)
  waiting for transfers between devices: 1520 us -> 0 us
  Pallas kernels: 0 us -> 332 us
  blocking collectives: 92.8 us -> 0 us
  local copies, waits for them, and re-layouts: 64.8 us -> 105 us
  other arithmetic: 8.64 us -> 38.6 us
    reduce_scatter x2 -> x0, waiting for transfers between devices: 854 us -> none  [the longest x1 473 us: per_device(): lax.psum_scatter(blocks[2], ('rep', 'grp'), scatter_dimension=0, tiled=True)]
    all_gather x7 -> x0, waiting for transfers between devices: 439 us -> none  [the longest x1 137 us: per_device(): lax.all_gather(expand_weight, 'grp', axis=1, tiled=True)]
    pallas_call x0 -> x2, Pallas kernels: none -> 332 us  [the longest x1 201 us: reduce_all(): pl.pallas_call(functools.partial(reduce_kernel, R, G, share, con_count, e...]
    unnamed x13 -> x0, waiting for transfers between devices: 221 us -> none
    dot_general x12 -> x2, matrix products: 64.5 us -> 8.71 us  [dot_nt(): lax.dot_general(left, right, (((1,), (1,)), ((), ())), preferred_element_...]
    dot_general x6 -> x12, matrix products: 7.08 us -> 55.8 us  [product(): return jnp.einsum(form, left, right, preferred_element_type=jnp.float32)]
    unnamed x1 -> x0, blocking collectives: 42.2 us -> none
    psum x1 -> x0, blocking collectives: 41.4 us -> none  [per_device(): lax.psum((vectors[0], vectors[1], vectors[2], vectors[3], vectors[4], vec...]
  transfers between devices with their start and end apart: 11 -> 0, of which waited for: 11 -> 0; matrix products, arithmetic and copies ran while one was open for 6% -> 0% of each run, Pallas kernels for 0% -> 0%
where the time goes in v1:
time: 547 us; the launch traced here: 542 us
  Pallas kernels  332 us (61%)
  local copies, waits for them, and re-layouts  105 us (19%)
  matrix products  64.5 us (12%)
  other arithmetic  38.6 us (7%)
    pallas_call x1, Pallas kernels, reduce_all(): pl.pallas_call(functools.partial(reduce_kernel, R, G, share, con_count, e...  201 us
    pallas_call x1, Pallas kernels, gather_all(): pl.pallas_call(functools.partial(gather_kernel, R, G, share, 2), out_shap...  131 us
    dot_general x12, matrix products, product(): return jnp.einsum(form, left, right, preferred_element_type=jnp.float32)  55.8 us
    transpose x2, local copies, waits for them, and re-layouts, per_device(): con_t = jnp.swapaxes(gathered[:, 4 + Q:], 0, 1).reshape(Q, D, D)  23.4 us
    unnamed x85, local copies, waits for them, and re-layouts  12.2 us

profile of v1, /device:TPU:0, one launch (start us, length us, event | category | flops | bytes accessed | tf_op | source)
XLA Modules:
  0.0 541.7 jit_solution(8919199840667543776)
XLA Ops:
  0.7 0.9 reduce-window.4
  3.6 1.4 reduce_sum.184
  5.0 6.1 %concatenate.32 = bf16[1632]{0:T(1024)(128)(2,1)S(1)} concatenate(bf16[136]{0:T(256)(128)(2,1)} %param.19, bf16[136]{0:T(256)(128)(2,1)} %param.20, bf16[136]{0:T(256)(128)(2,1)} %param.22, bf16[136]{0:T(256)(128)(2,1)} %param.23, bf16[136]{0:T(256)(128)(2,1)} %param.25, bf16[136]{0:T(256)(128)(2,1)} %param.26, bf16[136]{0:T(256)(128)(2,1)} %param.27, bf16[136]{0:T(256)(128)(2,1)} %param.31, ...), dimensions={0} | concatenate | bytes 6528 | tf_op jit(solution)/shard_map/concatenate | solution.py:855
  11.7 0.7 fusion.30
  12.4 1.6 copy.133
  15.6 1.1 copy.152
  16.7 4.0 reshape.301
  20.6 1.5 copy.181
  22.3 4.0 pad_maximum_fusion.2.own_ref
  26.3 131.5 %gather_all.1 = (bf16[8,12,136,1088]{3,2,1,0:T(8,128)(2,1)}, bf16[8,16,128]{2,1,0:T(8,128)(2,1)}) custom-call(bf16[12,136,1088]{2,1,0:T(8,128)(2,1)} %pad_maximum_fusion.2.own_ref, bf16[16,128]{1,0:T(8,128)(2,1)} %pad_bitcast_fusion.1.small_ref), custom_call_target="tpu_custom_call" | custom-call | tf_op jit(solution)/shard_map/gather_all/pallas_call | solution.py:350
  157.7 0.8 copy.182
  158.6 0.7 reshape.328
  159.4 0.7 reshape.329
  161.0 0.7 reshape.325
  161.9 3.4 slice.73
  165.3 6.7 %slice.67 = bf16[8,3,136,1088]{3,2,1,0:T(8,128)(2,1)} slice(bf16[8,12,136,1088]{3,2,1,0:T(8,128)(2,1)} %get-tuple-element.20), slice={[0:8], [0:3], [0:136], [0:1088]} | slice | bytes 14204928 | tf_op jit(solution)/shard_map/slice | solution.py:866
  172.0 14.9 %slice_bitcast_fusion = (bf16[4,8,136,1088]{3,2,0,1:T(8,128)(2,1)}, bf16[8,4,136,1088]{3,2,1,0:T(8,128)(2,1)}) fusion(bf16[8,12,136,1088]{3,2,1,0:T(8,128)(2,1)} %get-tuple-element.20), kind=kLoop, calls=%fused_computation | loop fusion | bytes 37879808 | tf_op jit(solution)/shard_map/transpose | solution.py:869
  186.9 8.6 %copy.137 = bf16[4,8,136,1088]{3,2,1,0:T(8,128)(2,1)} copy(bf16[4,8,136,1088]{3,2,0,1:T(8,128)(2,1)} %get-tuple-element.93) | data formatting | bytes 18939904 | tf_op jit(solution)/shard_map/transpose | solution.py:869
  195.5 5.8 %fusion = bf16[256,3264]{0,1:T(8,128)(2,1)S(1)} fusion(bf16[3264,1088]{1,0:T(8,128)(2,1)} %bitcast.172, f32[3264]{0:T(1024)S(1)} %concatenate.33, f32[256,1088]{1,0:T(8,128)S(1)} %copy-done.1, f32[1088]{0:T(1024)S(1)} %reshape.322, f32[1088]{0:T(1024)S(1)} %reshape.321, f32[256]{0:T(256)S(1)} %copy-done.33, f32[256]{0:T(256)S(1)} %copy-done.31), kind=kOutput, calls=%fused_computation.6 | convolution fusion | flops 1821294592 | bytes 9911552 | tf_op jit(solution)/shard_map/dot_general | solution.py:804
  201.8 5.2 fusion.25
  207.1 0.9 fusion.19
  208.0 0.9 exponential_reduce_fusion
  209.0 1.2 convolution_convert_fusion.2
  210.2 0.8 copy-done.17
  211.0 1.1 copy.156
  212.1 3.0 fusion.47
  216.5 5.9 %copy.143 = f32[4,1088,256]{1,2,0:T(8,128)} copy(f32[4,1088,256]{2,1,0:T(8,128)} %fusion.25) | data formatting | bytes 8912896 | tf_op jit(solution)/shard_map/tn,qnk->qtk/dot_general | solution.py:35
  222.3 10.5 %fusion.17 = (bf16[4,1088,256]{2,1,0:T(8,128)(2,1)S(1)}, f32[4,1088,256]{2,1,0:T(8,128)}) fusion(f32[4,1088,256]{2,1,0:T(8,128)} %fusion.25, f32[4,1088]{1,0:T(4,128)} %reshape.328, bf16[4,1088,1088]{2,1,0:T(8,128)(2,1)} %bitcast.165, f32[1088]{0:T(1024)} %reshape.327, f32[1088]{0:T(1024)S(1)} %reshape.326, f32[256]{0:T(256)} %add_rsqrt_fusion, ...), kind=kOutput, calls=%fused_computation.28 | convolution fusion | flops 2449096704 | bytes 21753344 | tf_op jit(solution)/shard_map/tk,qnk->qtn/dot_general | solution.py:35
  232.8 1.5 copy.153
  234.3 5.8 %copy.136 = f32[4,1088,256]{1,2,0:T(8,128)} copy(f32[4,1088,256]{2,1,0:T(8,128)} %get-tuple-element.130) | data formatting | bytes 8912896 | tf_op jit(solution)/shard_map/add | solution.py:890
  240.1 8.1 %fusion.41 = (f32[4,1088]{1,0:T(4,128)}, bf16[4,256,1088]{2,1,0:T(8,128)(2,1)}, bf16[4,256,1088]{2,1,0:T(8,128)(2,1)S(1)}) fusion(f32[4,1088,256]{1,2,0:T(8,128)} %copy.136, f32[4,1088,256]{1,2,0:T(8,128)} %copy.143), kind=kLoop, calls=%fused_computation.115 | loop fusion | flops 25620224 | bytes 13386752 | tf_op jit(solution)/shard_map/reduce_sum | solution.py:923
  248.2 1.4 copy-done.9
  249.6 8.1 %fusion.23 = f32[256,1088]{1,0:T(8,128)} fusion(f32[256,1088]{1,0:T(8,128)S(1)} %get-tuple-element.126, bf16[4,256,1088]{2,1,0:T(8,128)(2,1)S(1)} %get-tuple-element.97, bf16[4,1088,1088]{2,1,0:T(8,128)(2,1)} %bitcast.167, f32[1088]{0:T(1024)S(1)} %copy-done.34, pred[256]{0:T(512)(128)(4,1)S(1)} %copy-done.37), kind=kOutput, calls=%fused_computation.43 | convolution fusion | flops 2425143296 | bytes 13931008 | tf_op jit(solution)/shard_map/qtk,qnk->tn/dot_general | solution.py:35
  257.8 2.6 copy.160
  260.4 10.3 %fusion.49 = (f32[1088]{0:T(1024)}, f32[256,1088]{0,1:T(8,128)}) fusion(bf16[4,1088,1088]{2,1,0:T(8,128)(2,1)} %bitcast.166, bf16[4,256,1088]{2,1,0:T(8,128)(2,1)} %get-tuple-element.90), kind=kOutput, calls=%fused_computation.122 | convolution fusion | flops 2424585216 | bytes 12816640 | tf_op jit(solution)/shard_map/qtn,qnk->tk/dot_general | solution.py:35
  270.7 1.4 reshape.315
  272.1 2.6 copy.146
  274.8 3.3 multiply_reduce_fusion
  278.1 2.6 fusion.43
  280.7 1.2 convolution_convert_fusion
  282.3 2.0 fusion.44
  284.3 2.9 multiply_convert_fusion
  287.9 2.7 convolution_convert_fusion.1
  290.5 2.4 fusion.45
  293.6 8.4 %fusion.48 = (f32[1088]{0:T(1024)}, f32[256,1088]{0,1:T(8,128)}) fusion(bf16[3264,1088]{1,0:T(8,128)(2,1)} %bitcast.173, bf16[256,1088]{0,1:T(8,128)(2,1)} %bitcast.198, bf16[256,1088]{0,1:T(8,128)(2,1)} %bitcast.183, bf16[256,1088]{0,1:T(8,128)(2,1)} %bitcast.185), kind=kOutput, calls=%fused_computation.121 | convolution fusion | flops 1823521792 | bytes 9892096 | tf_op jit(solution)/shard_map/tn,nk->tk/dot_general | solution.py:35
  302.1 1.3 copy.155
  303.4 1.7 copy.151
  305.1 2.7 multiply_reduce_fusion.1
  307.8 1.5 concatenate.41
  309.3 1.4 pad_bitcast_fusion.vec_ref
  310.8 0.7 broadcast_multiply_fusion
  311.5 0.7 broadcast_multiply_fusion.1
  312.1 2.3 convert_bitcast_fusion
  314.5 1.3 copy.154
  315.8 4.3 pad_maximum_fusion.dy_ref
  320.5 2.3 pad_maximum_fusion.1.x_ref
  322.8 200.6 %reduce_all.1 = (f32[12,136,1088]{2,1,0:T(8,128)}, f32[104,128]{1,0:T(8,128)}, f32[1,1,8,128]{3,2,1,0:T(8,128)}) custom-call(bf16[9,4,2,136,256]{4,3,2,1,0:T(8,128)(2,1)} %pad_maximum_fusion.dy_ref, bf16[7,256,1088]{2,1,0:T(8,128)(2,1)} %pad_maximum_fusion.1.x_ref, f32[104,128]{1,0:T(8,128)} %pad_bitcast_fusion.vec_ref), custom_call_target="tpu_custom_call" | custom-call | tf_op jit(solution)/shard_map/reduce_all/pallas_call | solution.py:750
  523.4 1.4 dynamic_slice.34
  524.7 1.5 fusion.46
  526.2 1.9 slice_bitcast_fusion.2
  528.2 2.6 copy.161
  530.8 2.9 slice.81
  533.6 4.2 slice_bitcast_fusion.1
  538.5 3.0 reshape.320
  (109 shorter events, 10.4 us)
Async XLA Ops:
  0.7 14.4 %copy-start.20 = (f32[256,1088]{0,1:T(8,128)S(1)}, f32[256,1088]{0,1:T(8,128)}, u32[]{:S(2)}) copy-start(f32[256,1088]{0,1:T(8,128)} %param.18) | copy-start | bytes 3342340
  2.8 12.6 %copy-start.35 = (pred[256]{0:T(512)(128)(4,1)}, pred[256]{0:T(512)(128)(4,1)S(1)}, u32[]{:S(2)}) copy-start(pred[256]{0:T(512)(128)(4,1)S(1)} %iota_compare_fusion.2) | copy-start | bytes 772
  5.0 9.3 %copy-start.30 = (f32[256]{0:T(256)}, f32[256]{0:T(256)S(1)}, u32[]{:S(2)}) copy-start(f32[256]{0:T(256)S(1)} %broadcast_multiply_fusion.5) | copy-start | bytes 3076
  14.1 1.5 copy-start
  15.4 5.2 copy-start.3
  16.7 5.5 %copy-start.21 = (bf16[1088,408]{0,1:T(8,128)(2,1)S(1)}, bf16[1088,408]{0,1:T(8,128)(2,1)}, u32[]{:S(2)}) copy-start(bf16[1088,408]{0,1:T(8,128)(2,1)} %param.21) | copy-start | bytes 2663428
  16.7 5.5 %copy-start.25 = (bf16[1088,136]{0,1:T(8,128)(2,1)S(1)}, bf16[1088,136]{0,1:T(8,128)(2,1)}, u32[]{:S(2)}) copy-start(bf16[1088,136]{0,1:T(8,128)(2,1)} %param.24) | copy-start | bytes 887812
  20.6 1.7 copy-start.19
  161.0 34.5 %copy-start.27 = (f32[1088]{0:T(1024)}, f32[1088]{0:T(1024)S(1)}, u32[]{:S(2)}) copy-start(f32[1088]{0:T(1024)S(1)} %reshape.322) | copy-start | bytes 13060
  186.8 8.6 %copy-start.1 = (f32[256,1088]{1,0:T(8,128)S(1)}, f32[256,1088]{1,0:T(8,128)}, u32[]{:S(2)}) copy-start(f32[256,1088]{1,0:T(8,128)} %copy-done) | copy-start | bytes 3342340
  186.8 8.6 %copy-start.31 = (f32[256]{0:T(256)S(1)}, f32[256]{0:T(256)}, u32[]{:S(2)}) copy-start(f32[256]{0:T(256)} %copy-done.30) | copy-start | bytes 3076
  186.8 8.6 %copy-start.33 = (f32[256]{0:T(256)S(1)}, f32[256]{0:T(256)}, u32[]{:S(2)}) copy-start(f32[256]{0:T(256)} %add_rsqrt_fusion.1) | copy-start | bytes 3076
  195.5 5.8 %copy-start.4 = (f32[256,1088]{1,0:T(8,128)S(1)}, f32[256,1088]{1,0:T(8,128)}, u32[]{:S(2)}) copy-start(f32[256,1088]{1,0:T(8,128)} %copy-done.3) | copy-start | bytes 3342340
  195.5 6.4 %copy-start.7 = (bf16[4,8,136,1088]{3,2,1,0:T(8,128)(2,1)S(1)}, bf16[4,8,136,1088]{3,2,1,0:T(8,128)(2,1)}, u32[]{:S(2)}) copy-start(bf16[4,8,136,1088]{3,2,1,0:T(8,128)(2,1)} %copy.137) | copy-start | bytes 28409860
  195.5 6.3 %copy-start.36 = (pred[256]{0:T(512)(128)(4,1)S(1)}, pred[256]{0:T(512)(128)(4,1)}, u32[]{:S(2)}) copy-start(pred[256]{0:T(512)(128)(4,1)} %copy-done.35) | copy-start | bytes 772
  201.3 7.7 %copy-start.11 = (bf16[256,3264]{0,1:T(8,128)(2,1)}, bf16[256,3264]{0,1:T(8,128)(2,1)S(1)}, u32[]{:S(2)}) copy-start(bf16[256,3264]{0,1:T(8,128)(2,1)S(1)} %fusion) | copy-start | bytes 5013508
  201.8 5.3 copy-start.22
  208.0 2.2 copy-start.2
  209.0 1.2 copy-start.28
  210.2 0.8 copy-start.17
  215.1 0.6 copy-start.32
  240.1 9.5 %copy-start.34 = (f32[1088]{0:T(1024)S(1)}, f32[1088]{0:T(1024)}, u32[]{:S(2)}) copy-start(f32[1088]{0:T(1024)} %reshape.329) | copy-start | bytes 13060
  240.1 9.5 %copy-start.37 = (pred[256]{0:T(512)(128)(4,1)S(1)}, pred[256]{0:T(512)(128)(4,1)}, u32[]{:S(2)}) copy-start(pred[256]{0:T(512)(128)(4,1)} %copy-done.35) | copy-start | bytes 772
  248.2 1.4 copy-start.9
  274.8 7.5 %slice-start = ((s8[4456448]{0:T(1024)(128)(4,1)}), s8[4194304]{0:T(1024)(128)(4,1)S(1)}, s32[]{:S(2)}) async-start(s8[4456448]{0:T(1024)(128)(4,1)} %bitcast.163), calls=%async_computation | async-start | bytes 8388608
  278.1 2.6 copy-start.8
  278.1 4.2 slice-start.1
  280.6 1.6 copy-start.5
  280.6 1.4 copy-start.18
  280.7 1.7 copy-start.23
  280.7 1.7 copy-start.29
  293.6 8.4 %copy-start.15 = (bf16[17,64,256]{2,1,0:T(8,128)(2,1)S(1)}, bf16[17,64,256]{2,1,0:T(8,128)(2,1)}, u32[]{:S(2)}) copy-start(bf16[17,64,256]{2,1,0:T(8,128)(2,1)} %convolution_convert_fusion.1) | copy-start | bytes 1671172
  293.6 8.4 %copy-start.16 = (bf16[256,17,64]{0,2,1:T(8,128)(2,1)S(1)}, bf16[256,17,64]{0,2,1:T(8,128)(2,1)}, u32[]{:S(2)}) copy-start(bf16[256,17,64]{0,2,1:T(8,128)(2,1)} %get-tuple-element.106) | copy-start | bytes 1671172
  293.6 8.4 %copy-start.24 = (bf16[256,17,64]{0,2,1:T(8,128)(2,1)S(1)}, bf16[256,17,64]{0,2,1:T(8,128)(2,1)}, u32[]{:S(2)}) copy-start(bf16[256,17,64]{0,2,1:T(8,128)(2,1)} %get-tuple-element.104) | copy-start | bytes 1671172
  303.4 4.4 copy-start.26
  303.4 8.8 %copy-start.6 = (f32[256,1088]{1,0:T(8,128)S(1)}, f32[256,1088]{1,0:T(8,128)}, u32[]{:S(2)}) copy-start(f32[256,1088]{1,0:T(8,128)} %copy-done.5) | copy-start | bytes 3342340
  315.7 4.4 copy-start.10
  315.8 4.3 copy-start.12
  315.8 4.3 copy-start.13
  315.8 4.7 copy-start.14

commit v2 on v0

v2 whole, which is shorter than its diff:
```python
import functools
import types

import jax
import jax.numpy as jnp
from jax import lax
from jax.experimental import pallas as pl
from jax.experimental.pallas import tpu as pltpu
from jax.sharding import PartitionSpec as P

HD = 64
EPSILON = 1e-05
MASKED = -1e30
PAD = 8
YSIZE = 2
TEAM = 4
GELU_A = 0.7978845608028654
GELU_B = 0.044715
MESH_ID = pl.DeviceIdType.MESH
VMEM_LIMIT = 67043328
BF16, F32 = jnp.bfloat16, jnp.float32


def bits_of(count):
    return count.bit_length() - 1


def dot_nn(left, right):
    return lax.dot_general(left, right, (((1,), (0,)), ((), ())), preferred_element_type=F32)


def dot_nt(left, right):
    return lax.dot_general(left, right, (((1,), (1,)), ((), ())), preferred_element_type=F32)


def dot_tn(left, right):
    return lax.dot_general(left, right, (((0,), (0,)), ((), ())), preferred_element_type=F32)


def remote(src, dst, send, recv, target):
    return pltpu.make_async_remote_copy(
        src_ref=src, dst_ref=dst, send_sem=send, recv_sem=recv, device_id=target, device_id_type=MESH_ID
    )


def wide(value):
    return value.astype(F32)


def low(value):
    return value.astype(BF16)


class Place:
    def __init__(self, rep_count, grp_count):
        self.R, self.G = rep_count, grp_count
        self.Z = grp_count // YSIZE
        self.r = lax.axis_index("rep")
        self.g = lax.axis_index("grp")
        self.c = self.r % 2
        self.xi = (self.r // 2) % 2
        self.q = self.r % TEAM
        self.z = self.g // YSIZE
        self.y = self.g % YSIZE
        self.partner = (self.r + 1 - 2 * self.c, self.g)
        self.xnbr = (self.r + 2 - 4 * self.xi, self.g)
        self.ynbr = (self.r, self.g + 1 - 2 * self.y)
        self.up = (self.r, self.g + YSIZE)
        self.down = (self.r, self.g - YSIZE)
        self.q_partner = self.q + 1 - 2 * self.c
        self.q_x = self.q + 2 - 4 * self.xi
        self.q_far = self.q_x + 1 - 2 * self.c

    def on_line(self, zz):
        return (self.r, zz * YSIZE + self.y)

    def flip_rep(self, bit):
        on = (self.r // (1 << bit)) % 2
        return (self.r + (1 << bit) - (2 << bit) * on, self.g)

    def flip_grp(self, bit):
        on = (self.g // (1 << bit)) % 2
        return (self.r, self.g + (1 << bit) - (2 << bit) * on)


def greet(here, others):
    barrier = pltpu.get_barrier_semaphore()

    def hello(target):
        pl.semaphore_signal(barrier, inc=1, device_id=target, device_id_type=MESH_ID)

    for target in [here.partner, here.xnbr, here.ynbr] + others:
        hello(target)
    for zz in range(here.Z):

        @pl.when(here.z != zz)
        def _(zz=zz):
            hello(here.on_line(zz))

    pl.semaphore_wait(barrier, 2 + here.Z + len(others))


def loop(count, body):
    def step(i, carry):
        body(i)
        return carry

    lax.fori_loop(0, count, step, 0)


def layer_kernel(R, G, give_in, give_out, names, *refs):
    len_ref, tok_ref, cot_ref, ain_ref, aout_ref, exp_ref, con_ref = refs[:7]
    vector_refs = refs[7:16]
    bo_out, tg_out, grad_out, con_out, vec_out, con_cut, yb_a, zb_a, deep_buf = refs[16:25]
    s = types.SimpleNamespace(**dict(zip(names, refs[25:])))
    here = Place(R, G)
    Z, z, y, c, xi, q, g = here.Z, here.z, here.y, here.c, here.xi, here.q, here.g
    D, T = tok_ref.shape
    n = D // G
    H = D // HD
    Q = TEAM
    FF = con_ref.shape[1]
    n4 = Q * n
    B = 2 * n
    scale = HD ** (-0.5)
    rep_bits, grp_bits = bits_of(R), bits_of(G)
    rounds = rep_bits + grp_bits
    w_io, w_ffn = s.w_io, s.w_ffn
    ioT, xo, xp, projT, resT = s.ioT, s.xo, s.xp, s.projT, s.resT
    h24, st4, brT = s.h24, s.st4, s.brT
    dyp, ps, pS, prb, xrb, accP = s.dyp, s.ps, s.pS, s.prb, s.xrb, s.accP
    lse, maskb, live, vecT = s.lse, s.maskb, s.live, s.vecT
    vec_buf, vec_got = s.vec_buf, s.vec_got
    gk, gs, yb_f, zb_f = s.gk, s.gs, s.yb_f, s.zb_f
    xb, fx, small_all = s.xb, s.fx, s.small_all

    N = 4
    wide_in = n - give_in
    start_in = xi * give_in
    giving = xi * wide_in
    taking = (1 - xi) * wide_in

    def io_row(k, gg):
        return jnp.where(k < 3, 3 * n * gg + n * k, 3 * D + n * gg)

    first_y = (3 * n // 17) // 8 * 8

    def rows(base, offset, size):
        return pl.ds(pl.multiple_of(base + offset, 8), size)

    def plane_w(k, gg):
        return w_io.at[rows(io_row(k, gg), start_in, wide_in), :]

    def gift_w(k, gg):
        return w_io.at[rows(io_row(k, gg), giving, give_in), :]

    def due_w(k, gg):
        return w_io.at[rows(io_row(k, gg), taking, give_in), :]

    def shard(zz, yy):
        return zz * YSIZE + yy

    def farthest(i):
        table = [sorted(range(Z), key=lambda p: -abs(p - at)) for at in range(Z)]
        pick = jnp.int32(0)
        for at in range(Z):
            for j in range(Z):
                pick = jnp.where((z == at) & (i == j), table[at][j], pick)
        return pick

    def goes_on(zz):
        return ((zz < z) & (z < Z - 1)) | ((zz > z) & (z > 0))

    source = y == c
    onward_of = lambda zz: (here.r, g + jnp.where(zz < z, YSIZE, -YSIZE))

    def own_copy(k, way):
        ref = plane_w(k, g)
        return remote(ref, ref, s.a_own.at[k, way], s.a_rp.at[k, z], (here.up, here.down, here.ynbr)[way])

    def passing(k, zz):
        ref = plane_w(k, shard(zz, y))
        return remote(ref, ref, s.a_fwd.at[k, zz], s.a_rp.at[k, zz], onward_of(zz))

    def over_y(k, zz, yy):
        ref = plane_w(k, shard(zz, yy))
        return remote(ref, ref, s.a_y.at[k, zz], s.a_rp.at[k, zz], here.ynbr)

    def over_x(k, zz):
        ref = gift_w(k, shard(zz, c))
        return remote(ref, ref, s.a_x.at[k, zz], s.a_rx.at[k, zz], here.xnbr)

    def x_arrival(k, zz):
        ref = due_w(k, shard(zz, c))
        return remote(ref, ref, s.a_x.at[k, zz], s.a_rx.at[k, zz], here.xnbr)

    def plane_to_partner(k, zz, core):
        ref = plane_w(k, shard(zz, core))
        return remote(ref, ref, s.a_cp.at[k, zz], s.a_rcp.at[k, zz], here.partner)

    def rest_to_partner(k, zz, core):
        ref = due_w(k, shard(zz, core))
        return remote(ref, ref, s.a_cx.at[k, zz], s.a_rcx.at[k, zz], here.partner)

    def ffn_w(mt, gg):
        return w_ffn.at[mt, rows(n * gg, 0, n), :]

    def ffn_own(mt, way):
        ref = ffn_w(mt, g)
        return remote(ref, ref, s.w_own.at[mt, way], s.w_rz.at[mt, z], (here.up, here.down, here.ynbr)[way])

    def ffn_own_y(mt):
        ref = ffn_w(mt, g)
        return remote(ref, ref, s.w_own.at[mt, 2], s.w_ry.at[mt, z], here.ynbr)

    def ffn_pass(mt, zz):
        ref = ffn_w(mt, shard(zz, y))
        return remote(ref, ref, s.w_fwd.at[mt, zz], s.w_rz.at[mt, zz], onward_of(zz))

    def ffn_over_y(mt, zz, yy):
        ref = w_ffn.at[mt, rows(n * shard(zz, yy), 0, n - first_y), :]
        return remote(ref, ref, s.w_y.at[mt, zz], s.w_ry.at[mt, zz], here.ynbr)

    def ffn_own_y_arrival(mt):
        ref = ffn_w(mt, shard(z, 1 - y))
        return remote(ref, ref, s.w_own.at[mt, 2], s.w_ry.at[mt, z], here.ynbr)

    def ffn_edge(mt, zz):
        return w_ffn.at[mt, rows(n * shard(zz, 1 - y), n - first_y, first_y), :]

    def edge_own(mt, way):
        ref = ffn_edge(mt, z)
        return remote(ref, ref, s.u_own.at[mt, way], s.u_rz.at[mt, z], (here.up, here.down)[way])

    def edge_pass(mt, zz):
        ref = ffn_edge(mt, zz)
        return remote(ref, ref, s.u_fwd.at[mt, zz], s.u_rz.at[mt, zz], onward_of(zz))

    def start_own(k):
        @pl.when(source)
        def _():
            @pl.when(z < Z - 1)
            def _():
                own_copy(k, 0).start()

            @pl.when(z > 0)
            def _():
                own_copy(k, 1).start()

            own_copy(k, 2).start()

    def start_ffn(mt):
        @pl.when(z < Z - 1)
        def _():
            ffn_own(mt, 0).start()

        @pl.when(z > 0)
        def _():
            ffn_own(mt, 1).start()

    def start_ffn_y(mt):
        ffn_own_y(mt).start()

    def both_sides(distance, act):
        def side(i):
            zz = z + jnp.where(i == 0, -distance, distance)

            @pl.when((zz >= 0) & (zz < Z) & ((i == 0) | (distance > 0)))
            def _():
                act(zz)

        loop(2, side)

    def gather_wave(d, part):
        def plane_step(j):
            k = 3 * part + j

            @pl.when((k < N) & source & (d > 0))
            def _():
                def arrived(zz):
                    passing(k, zz).wait_recv()

                    @pl.when(goes_on(zz))
                    def _():
                        passing(k, zz).start()

                    over_y(k, zz, y).start()
                    over_x(k, zz).start()
                    plane_to_partner(k, zz, c).start()

                both_sides(d, arrived)

            @pl.when((k < N) & (y != c))
            def _():
                def arrived(zz):
                    over_y(k, zz, c).wait_recv()
                    over_x(k, zz).start()
                    plane_to_partner(k, zz, c).start()

                both_sides(d, arrived)

        def x_step(j):
            k = 3 * part + j

            @pl.when((k < N) & ((d > 1) | ((d > 0) & (y != c))))
            def _():
                def arrived(zz):
                    x_arrival(k, zz).wait_recv()
                    rest_to_partner(k, zz, c).start()

                both_sides(d - 1, arrived)

        loop(3, plane_step)
        loop(3, x_step)

    def partner_arrivals(k):
        def each(zz):
            @pl.when((y == c) | (zz != z))
            def _():
                plane_to_partner(k, zz, 1 - c).wait_recv()
                rest_to_partner(k, zz, 1 - c).wait_recv()

        loop(Z, each)

    def ffn_wave(mt, d):
        def arrived(zz):
            ffn_pass(mt, zz).wait_recv()

            @pl.when(goes_on(zz))
            def _():
                ffn_pass(mt, zz).start()

            ffn_over_y(mt, zz, y).start()

        both_sides(d, arrived)

    def ffn_edges(mt, d):
        @pl.when(d == 0)
        def _():
            ffn_own_y_arrival(mt).wait_recv()

            @pl.when(z < Z - 1)
            def _():
                edge_own(mt, 0).start()

            @pl.when(z > 0)
            def _():
                edge_own(mt, 1).start()

        @pl.when(d > 0)
        def _():
            def arrived(zz):
                edge_pass(mt, zz).wait_recv()

                @pl.when(goes_on(zz))
                def _():
                    edge_pass(mt, zz).start()

            both_sides(d, arrived)

    def ffn_y_arrivals(mt):
        def each(zz):
            @pl.when(zz != z)
            def _():
                ffn_over_y(mt, zz, 1 - y).wait_recv()

        loop(Z, each)

    def share_copy(e, buf, kind):
        slot = (q, q, here.q_x)[kind]
        target = (here.partner, here.xnbr, here.partner)[kind]
        ref = buf.at[slot]
        return remote(ref, ref, s.e_send.at[e, kind], s.e_recv.at[e, kind], target)

    def share_arrival(e, buf, kind):
        slot = (here.q_partner, here.q_x, here.q_far)[kind]
        target = (here.partner, here.xnbr, here.partner)[kind]
        ref = buf.at[slot]
        return remote(ref, ref, s.e_send.at[e, kind], s.e_recv.at[e, kind], target)

    def swap_copy(i):
        return remote(xo.at[i], xp.at[i], s.p_send.at[i], s.p_recv.at[i], here.partner)

    def part_to_partner(e, j):
        return remote(ps.at[j], prb.at[e, j], s.r_send.at[e, j], s.r_recv.at[e, j], here.partner)

    def part_to_x(e):
        return remote(pS, xrb.at[e], s.r_send.at[e, 2], s.r_recv.at[e, 2], here.xnbr)

    def small_copy(bit, mine):
        size = 1 << bit
        base = (g // size) * size
        if not mine:
            base = base + size - 2 * size * ((g // size) % 2)
        ref = small_all.at[rows(n * base, 0, n * size), :]
        return remote(ref, ref, s.s_send.at[bit], s.s_recv.at[bit], here.flip_grp(bit))

    def fy_copy(mt, zz):
        return remote(gs.at[mt, zz], yb_f.at[mt, zz], s.fy_send.at[mt, zz], s.fy_recv.at[mt, zz], here.ynbr)

    def fz_copy(mt, zz):
        return remote(
            gk.at[mt, zz], zb_f.at[mt, z], s.fz_send.at[mt, zz], s.fz_recv.at[mt, z], here.on_line(zz)
        )

    def fz_arrival(mt, zz):
        return remote(
            gk.at[mt, zz], zb_f.at[mt, zz], s.fz_send.at[mt, zz], s.fz_recv.at[mt, zz], here.on_line(zz)
        )

    def piece(mt, which):
        return N + Q * mt + which

    def final_copy(mt, kind):
        target = (here.partner, here.xnbr, here.partner)[kind]
        slot = (q, q, here.q_x)[kind]
        src = grad_out.at[piece(mt, slot)] if kind == 2 else gk.at[mt, z]
        dst = grad_out.at[piece(mt, slot)]
        return remote(src, dst, s.fo_send.at[mt, kind], s.fo_recv.at[mt, kind], target)

    def final_arrival(mt, kind):
        target = (here.partner, here.xnbr, here.partner)[kind]
        slot = (here.q_partner, here.q_x, here.q_far)[kind]
        ref = grad_out.at[piece(mt, slot)]
        return remote(ref, ref, s.fo_send.at[mt, kind], s.fo_recv.at[mt, kind], target)

    def final_keep(mt):
        return pltpu.make_async_copy(gk.at[mt, z], grad_out.at[piece(mt, q)], s.fo_keep.at[mt])

    def deepen(ref, k):
        for bit in range(2, rep_bits):
            j = bit - 2
            give = remote(ref, deep_buf.at[k, j], s.d_send, s.d_recv.at[k, j], here.flip_rep(bit))
            give.start()
            give.wait()
            bring = pltpu.make_async_copy(deep_buf.at[k, j], s.d_tmp, s.d_local)
            bring.start()
            bring.wait()
            ref[...] = low(wide(ref[...]) + wide(s.d_tmp[...]))

    def ffn_grads(mt, left, right):
        def block(b):
            at = pl.ds(pl.multiple_of(b * B, 16), B)
            total = dot_nt(left[0, at, :], right[0])
            for t in range(1, Q):
                total = total + dot_nt(left[t, at, :], right[t])

            @pl.when(y == 0)
            def _():
                gk[mt, b] = low(total[:n])
                gs[mt, b] = low(total[n:])

            @pl.when(y == 1)
            def _():
                gk[mt, b] = low(total[n:])
                gs[mt, b] = low(total[:n])

            fy_copy(mt, b).start()

        loop(Z, lambda i: block(farthest(i)))

    def ffn_reduce_y(mt, i):
        zz = farthest(i)
        fy_copy(mt, zz).wait_recv()
        gk[mt, zz] = low(wide(gk[mt, zz]) + wide(yb_f[mt, zz]))

        @pl.when(zz != z)
        def _():
            fz_copy(mt, zz).start()

    def ffn_reduce_own(mt):
        total = wide(gk[mt, z])
        for i in range(Z - 1):
            zz = farthest(i)
            fz_arrival(mt, zz).wait_recv()
            total = total + wide(zb_f[mt, zz])
        gk[mt, z] = low(total)
        deepen(gk.at[mt, z], piece(mt, 0))
        final_keep(mt).start()
        final_copy(mt, 0).start()
        final_copy(mt, 1).start()

    def ffn_reduce_far(mt):
        final_arrival(mt, 1).wait_recv()
        final_copy(mt, 2).start()

    def column(j, at=None):
        block = small_all[: D] if at is None else small_all[at, :]
        return wide(block)[:, j : j + 1]

    def statistics(values):
        center = values - jnp.mean(values, axis=0, keepdims=True)
        inverse = lax.rsqrt(jnp.mean(center * center, axis=0, keepdims=True) + EPSILON)
        return center * inverse, inverse

    def norm_back(upstream, normed, inverse, gain):
        scaled = upstream * gain
        return inverse * (
            scaled
            - jnp.mean(scaled, axis=0, keepdims=True)
            - normed * jnp.mean(scaled * normed, axis=0, keepdims=True)
        )

    def total_of(values):
        return jnp.sum(values, axis=1, keepdims=True)

    extra = [here.flip_rep(b) for b in range(2, rep_bits)]

    def schedule(steps):
        def body(at):
            for act in dict.fromkeys(step[0] for step in steps):
                slots = [(i, step[1:]) for i, step in enumerate(steps) if step[0] is act]
                hit = at == slots[0][0]
                for i, _ in slots[1:]:
                    hit = hit | (at == i)

                @pl.when(hit)
                def _(act=act, slots=slots):
                    picked = []
                    for j in range(len(slots[0][1])):
                        values = [args[j] for _, args in slots]
                        pick = jnp.int32(values[0])
                        if len(set(values)) > 1:
                            for (i, _), value in zip(slots[1:], values[1:]):
                                pick = jnp.where(at == i, value, pick)
                        picked.append(pick)
                    act(*picked)

        loop(len(steps), body)

    local = s.l_sem

    def pull_io(ref, i):
        return pltpu.make_async_copy(ref, ioT, local.at[i])

    def opening(raw_con, turned, cut, piece_con, raw_cot, small_rows, small_own):
        put_in = pltpu.make_async_copy(ain_ref, w_io.at[rows(3 * n * g, 0, 3 * n), :], local.at[0])
        put_out = pltpu.make_async_copy(aout_ref, w_io.at[rows(3 * D + n * g, 0, n), :], local.at[1])
        put_exp = pltpu.make_async_copy(
            exp_ref.at[rows(n * q, 0, n), :], w_ffn.at[0, rows(n * g, 0, n), :], local.at[2]
        )
        pull_con = pltpu.make_async_copy(con_ref, raw_con, local.at[3])
        pull_cot = pltpu.make_async_copy(cot_ref, raw_cot, local.at[4])
        pull_tok = pull_io(tok_ref, 5)
        put_in.start()
        put_out.start()
        pull_tok.start()
        put_exp.start()
        pull_cot.start()
        pull_con.start()
        small_rows[...] = jnp.zeros_like(small_rows)
        for j, ref in enumerate(vector_refs[:8]):
            small_rows[j : j + 1, :] = wide(ref[...]).reshape(1, n)
        expand_bias = wide(vector_refs[8][...]).reshape(1, Q * n)
        for j in range(Q):
            small_rows[8 + j : 9 + j, :] = expand_bias[:, j * n : (j + 1) * n]
        small_own[...] = low(small_rows[...].T)
        put_small = pltpu.make_async_copy(small_own, small_all.at[rows(n * g, 0, n), :], s.k_sem.at[0])
        put_small.start()
        greet(here, extra)
        put_in.wait()
        put_small.wait()
        small_copy(0, True).start()
        put_out.wait()
        put_exp.wait()
        ends = []
        end = 0
        for i in range(len_ref.shape[1]):
            end = end + len_ref[0, i]
            ends.append(end)

        def labels(position):
            number = jnp.zeros(position.shape, jnp.int32)
            for end in ends:
                number = number + jnp.where(position >= end, 1, 0)
            return jnp.where(position < ends[-1], number, len(ends) + position)

        def small_rounds(bit):
            for b in range(grp_bits):

                @pl.when(bit == b)
                def _(b=b):
                    small_copy(b, False).wait_recv()
                    if b + 1 < grp_bits:
                        small_copy(b + 1, True).start()

        def layout():
            query_slot = lax.broadcasted_iota(jnp.int32, (1, T), 1)
            key_slot = lax.broadcasted_iota(jnp.int32, (T, 1), 0)
            query_label, key_label = labels(query_slot), labels(key_slot)
            allowed = (key_slot <= query_slot) & (key_label == query_label)
            maskb[...] = jnp.where(allowed, 0.0, MASKED)
            live[...] = jnp.where(query_slot < ends[-1], 1.0, 0.0)

        def first_norm():
            pull_tok.wait()
            normed, _ = statistics(ioT[...])
            xo[1] = low(normed * column(0) + column(1))
            swap_copy(1).start()

        def upstream():
            pull_cot.wait()
            start = jnp.where(live[...] > 0.5, raw_cot[...], 0.0)
            st4[q] = low(start)
            vecT[...] = jnp.zeros_like(vecT)
            vecT[:, 7:8] = total_of(start)

        def share_start():
            share_copy(0, st4, 0).start()
            share_copy(0, st4, 1).start()

        def pass_start():
            share_arrival(0, st4, 1).wait_recv()
            share_copy(0, st4, 2).start()

        def con_block(gg):
            return pltpu.make_async_copy(
                turned.at[rows(Q * n * gg, n * q, n), :], cut.at[rows(n * gg, 0, n), :], s.k_sem.at[gg]
            )

        def cut_contract():
            pull_con.wait()
            turned[:FF] = raw_con[...].T
            loop(G, lambda gg: con_block(gg).start())
            loop(G, lambda gg: con_block(gg).wait())
            piece_con[...] = cut[:D].T
            put = pltpu.make_async_copy(piece_con, w_ffn.at[1, rows(n * g, 0, n), :], local.at[3])
            put.start()
            put.wait()

        def project():
            def block(b):
                at = pl.ds(pl.multiple_of(b * B, 16), B)
                projT[at, :] = low(dot_nn(w_io[at, :], xo[1]))

            def add_bias(first, j):
                def each(b):
                    at = pl.ds(pl.multiple_of(b * B, 16), B)
                    to = pl.ds(pl.multiple_of(first + b * B, 16), B)
                    projT[to, :] = low(dot_nn(w_io[to, :], xo[1]) + column(j, at))

                loop(D // B, each)

            add_bias(0, 2)
            loop(D // B, lambda b: block(b + D // B))
            add_bias(2 * D, 3)

        def head_forward(h):
            at = pl.multiple_of(h * HD, HD)
            query = projT[pl.ds(at, HD), :]
            key = projT[pl.ds(pl.multiple_of(D + at, HD), HD), :]
            value = projT[pl.ds(pl.multiple_of(2 * D + at, HD), HD), :]
            scores = dot_nn(low(wide(key).T), query) * scale + maskb[...]
            peak = jnp.max(scores, axis=0, keepdims=True)
            logsum = peak + jnp.log(jnp.sum(jnp.exp(scores - peak), axis=0, keepdims=True))
            lse[h] = logsum
            weights = low(jnp.exp(scores - logsum))
            xo[0, pl.ds(at, HD), :] = low(dot_nn(value, weights))

        steps = [(start_own, k) for k in range(3)] + [(small_rounds, 0), (layout,)]
        steps += [(gather_wave, 0, 0), (start_own, 3), (gather_wave, 1, 0), (small_rounds, 1), (cut_contract,)]
        steps += [(gather_wave, 2, 0), (start_ffn, 0)] + [(small_rounds, b) for b in range(2, grp_bits)]
        steps += [(first_norm,)] + [(gather_wave, i, 0) for i in range(3, Z)] + [(gather_wave, 0, 1), (gather_wave, 1, 1)]
        steps += [(start_ffn_y, 0), (gather_wave, Z, 0), (upstream,), (gather_wave, 2, 1)]
        steps += [(partner_arrivals, k) for k in range(3)] + [(ffn_wave, 0, 1), (gather_wave, 3, 1)]
        steps += [(project,), (ffn_edges, 0, 0), (gather_wave, 4, 1), (share_start,)]
        served = {
            2: [(ffn_wave, 0, 2)],
            5: [(ffn_edges, 0, 1)],
            8: [(start_ffn, 1)],
            10: [(ffn_edges, 0, 2)],
            13: [(ffn_wave, 0, 3), (start_ffn_y, 1)],
            15: [(ffn_edges, 0, 3)],
            16: [(pass_start,)],
        }
        for h in range(H):
            steps += [(head_forward, h)] + served.get(h, [])
        schedule(steps)

    pl.run_scoped(
        opening,
        pltpu.VMEM((n, FF), BF16),
        pltpu.VMEM((FF + PAD, n), BF16),
        pltpu.VMEM((D + PAD, n), BF16),
        pltpu.VMEM((n, D), BF16),
        pltpu.VMEM((D, T), F32),
        pltpu.VMEM((128, n), F32),
        pltpu.VMEM((n, 128), BF16),
    )
    swap_copy(0).start()
    partner_arrivals(3)

    def attention_out(b):
        at = pl.ds(pl.multiple_of(b * B, 16), B)
        to = pl.ds(pl.multiple_of(3 * D + b * B, 16), B)
        resT[at, :] = ioT[at, :] + dot_nn(w_io[to, :], xo[0]) + column(4, at)

    loop(D // B, attention_out)
    pull_io(cot_ref, 5).start()
    normed, _ = statistics(resT[...])
    h24[q] = low(normed * column(5) + column(6))
    share_copy(1, h24, 0).start()
    share_copy(1, h24, 1).start()

    def dy_rows(k, zz, core):
        gg = shard(zz, core)
        row = jnp.where(k == 0, 3 * D + n * gg, 3 * n * gg + n * (k - 1))
        return rows(row, 0, n)

    def dy_swap(k, zz):
        return remote(
            projT.at[dy_rows(k, zz, 1 - c), :],
            dyp.at[k, zz],
            s.dy_send.at[k, zz],
            s.dy_recv.at[k, zz],
            here.partner,
        )

    def middle(gp4, act4, bb4):
        def expand(t):
            def block(b):
                at = pl.ds(pl.multiple_of(b * B, 16), B)
                part = wide(small_all[at, :])
                bias = part[:, 8:9]
                for j in range(1, Q):
                    bias = jnp.where(q == j, part[:, 8 + j : 9 + j], bias)
                u = dot_nn(w_ffn[0, at, :], h24[t]) + bias
                th = jnp.tanh(GELU_A * (u + GELU_B * (u * u * u)))
                act4[t, at, :] = low(0.5 * u * (1.0 + th))
                gp4[t, at, :] = 0.5 * (1.0 + th) + (0.5 * GELU_A) * u * (1.0 - th * th) * (
                    1.0 + (3.0 * GELU_B) * (u * u)
                )

            loop(D // B, block)

        def expand_step(i):
            @pl.when(i == 1)
            def _():
                share_arrival(1, h24, 0).wait_recv()

            @pl.when(i == 2)
            def _():
                share_arrival(1, h24, 1).wait_recv()
                share_copy(1, h24, 2).start()

            @pl.when(i == 3)
            def _():
                share_arrival(1, h24, 2).wait_recv()

            expand(member(i))

        def gradients():
            share_arrival(0, st4, 0).wait_recv()
            share_arrival(0, st4, 2).wait_recv()
            ffn_grads(1, st4, act4)

        def member(i):
            first = jnp.where(i == 1, here.q_partner, q)
            return jnp.where(i == 2, here.q_x, jnp.where(i == 3, here.q_far, first))

        def back_step(i):
            t = member(Q - 1 - i)

            def block(b):
                at = pl.ds(pl.multiple_of(b * B, 16), B)
                value = accP[at, :] * gp4[t, at, :]
                bb4[t, at, :] = low(value)
                vecT[at, 12:13] = vecT[at, 12:13] + total_of(value)

            accP[...] = dot_tn(w_ffn[1, :D], st4[t])
            loop(D // B, block)
            accP[...] = dot_tn(w_ffn[0, :D], bb4[t])

            @pl.when(i == 0)
            def _():
                ps[1] = low(accP[...])
                part_to_partner(0, 1).start()

            @pl.when(i == 1)
            def _():
                part_to_partner(0, 1).wait_recv()
                pS[...] = low(accP[...] + wide(prb[0, 1]))
                part_to_x(0).start()

            @pl.when(i == 2)
            def _():
                ps[0] = low(accP[...])
                part_to_partner(0, 0).start()

        def expand_gradients():
            ffn_grads(0, bb4, h24)
            for j in range(2):
                part_to_partner(0, j).wait_send()

        def out_step(i):
            t = member(Q - 1 - i)
            brT[...] = dot_nn(w_ffn[1, :D], act4[t])

            @pl.when(i == 0)
            def _():
                ps[1] = low(brT[...])
                part_to_partner(1, 1).start()

            @pl.when(i == 1)
            def _():
                gp4[1] = brT[...]

            @pl.when(i == 2)
            def _():
                ps[0] = low(brT[...])
                part_to_partner(1, 0).start()

            @pl.when(i == 3)
            def _():
                gp4[0] = brT[...]

        steps = [(ffn_wave, 1, 1), (ffn_y_arrivals, 0), (expand_step, 0), (ffn_wave, 1, 2), (expand_step, 1)]
        steps += [(ffn_edges, 1, 0), (ffn_wave, 1, 3), (expand_step, 2), (ffn_edges, 1, 1), (expand_step, 3)]
        steps += [(ffn_edges, 1, 2), (gradients,), (ffn_edges, 1, 3), (ffn_y_arrivals, 1)]
        steps += [(back_step, 0), (back_step, 1), (ffn_reduce_y, 1, 0), (back_step, 2), (ffn_reduce_y, 1, 1)]
        steps += [(back_step, 3), (expand_gradients,), (ffn_reduce_y, 1, 2)] + [(out_step, i) for i in range(Q)]
        steps += [(ffn_reduce_y, 1, 3)]
        schedule(steps)
        part_to_partner(0, 0).wait_recv()
        part_to_x(0).wait_recv()
        back_hidden = accP[...] + wide(prb[0, 0]) + wide(xrb[0])
        normed, inverse = statistics(resT[...])
        vecT[:, 5:6] = total_of(back_hidden * normed)
        vecT[:, 6:7] = total_of(back_hidden)
        pull_io(cot_ref, 5).wait()
        start = jnp.where(live[...] > 0.5, ioT[...], 0.0)
        brT[...] = start + norm_back(back_hidden, normed, inverse, column(5))
        projT[pl.ds(3 * D, D), :] = low(brT[...])
        loop(Z, lambda zz: dy_swap(0, zz).start())
        pull_io(tok_ref, 5).start()
        part_to_x(0).wait_send()
        part_to_partner(1, 1).wait_recv()
        pS[...] = low(gp4[1] + wide(prb[1, 1]))
        part_to_x(1).start()
        resT[...] = resT[...] + gp4[0] + column(7)
        vecT[:, 4:5] = total_of(brT[...])

    pl.run_scoped(
        middle, pltpu.VMEM((Q, D, T), F32), pltpu.VMEM((Q, D, T), BF16), pltpu.VMEM((Q, D, T), BF16)
    )
    batt = xrb.at[0]
    batt[...] = low(dot_tn(w_io[pl.ds(3 * D, D), :], projT[pl.ds(3 * D, D), :]))

    def head_backward(h):
        at = pl.multiple_of(h * HD, HD)
        at_q = pl.ds(at, HD)
        at_k = pl.ds(pl.multiple_of(D + at, HD), HD)
        at_v = pl.ds(pl.multiple_of(2 * D + at, HD), HD)
        query, key, value, up = projT[at_q, :], projT[at_k, :], projT[at_v, :], batt[at_q, :]
        scores = dot_nn(low(wide(key).T), query) * scale + maskb[...]
        probability = jnp.exp(scores - lse[h])
        weights = low(probability)
        delta = jnp.sum(wide(up) * wide(xo[0, at_q, :]), axis=0, keepdims=True)
        flow = dot_nn(low(wide(value).T), up)
        slope = low(probability * (flow - delta) * scale)
        back_query = dot_nn(key, slope)
        back_value = dot_nt(up, weights)
        vecT[at_q, 2:3] = total_of(back_query)
        vecT[at_q, 3:4] = total_of(back_value)
        projT[at_k, :] = low(dot_nt(query, slope))
        projT[at_q, :] = low(back_query)
        projT[at_v, :] = low(back_value)

    wide_out = n - give_out

    def closing(plane, xs, stage, fin, con_in, con_turn, con_tall, con_flat, vec_own):
        def x_copy(k, zz):
            return remote(xs.at[k, zz], xb.at[k, zz], s.gx_send.at[k, zz], s.gx_recv.at[k, zz], here.xnbr)

        def y_copy(k, zz):
            return remote(plane.at[k, zz], yb_a.at[k, zz], s.gy_send.at[k, zz], s.gy_recv.at[k, zz], here.ynbr)

        def z_copy(k, zz):
            return remote(
                plane.at[k, zz], zb_a.at[k, z], s.gz_send.at[k, zz], s.gz_recv.at[k, z], here.on_line(zz)
            )

        def z_arrival(k, zz):
            return remote(
                plane.at[k, zz], zb_a.at[k, zz], s.gz_send.at[k, zz], s.gz_recv.at[k, zz], here.on_line(zz)
            )

        def f_copy(k):
            return remote(plane.at[k, z], fx.at[k], s.gf_send.at[k], s.gf_recv.at[k], here.xnbr)

        def o_keep(k):
            return pltpu.make_async_copy(fin.at[k % 2], grad_out.at[k], s.go_keep.at[k])

        def o_give(k):
            return remote(fin.at[k % 2], grad_out.at[k], s.go_send.at[k], s.go_recv.at[k], here.partner)

        def bring(src, slot):
            copy = pltpu.make_async_copy(src, stage.at[slot], s.st_sem.at[slot])
            copy.start()
            return copy

        def multiply(k):
            j = jnp.where(k == 0, 0, 1)

            @pl.when(k == 0)
            def _():
                swap_copy(0).wait_recv()
                swap_copy(1).wait_recv()


            def each(i):
                zz = farthest(i)
                dy_swap(k, zz).wait_recv()
                term = dot_nt(projT[dy_rows(k, zz, c), :], xo[j]) + dot_nt(dyp[k, zz], xp[j])

                @pl.when(xi == 0)
                def _():
                    plane[k, zz] = low(term[:wide_out])
                    xs[k, zz] = low(term[wide_out:])

                @pl.when(xi == 1)
                def _():
                    plane[k, zz] = low(term[give_out:])
                    xs[k, zz] = low(term[:give_out])

                x_copy(k, zz).start()

            loop(Z, each)

        def after_x(k):
            def each(i):
                zz = farthest(i)
                x_copy(k, zz).wait_recv()
                got = wide(xb[k, zz])

                @pl.when(xi == 0)
                def _():
                    plane[k, zz, :give_out] = low(wide(plane[k, zz, :give_out]) + got)

                @pl.when(xi == 1)
                def _():
                    edge = wide_out - give_out
                    plane[k, zz, edge:] = low(wide(plane[k, zz, edge:]) + got)

                @pl.when(y != c)
                def _():
                    y_copy(k, zz).start()

            loop(Z, each)

        def after_y(k):
            @pl.when(source)
            def _():
                def fetch(i):
                    zz = farthest(i)
                    y_copy(k, zz).wait_recv()
                    bring(yb_a.at[k, zz], i)

                def add(i):
                    zz = farthest(i)
                    pltpu.make_async_copy(yb_a.at[k, zz], stage.at[i], s.st_sem.at[i]).wait()
                    plane[k, zz] = low(wide(plane[k, zz]) + wide(stage[i]))

                    @pl.when(i < Z - 1)
                    def _():
                        z_copy(k, zz).start()

                def step(i):
                    @pl.when(i < Z)
                    def _():
                        fetch(i)

                    @pl.when(i > 0)
                    def _():
                        add(i - 1)

                loop(Z + 1, step)

        def after_z(k):
            @pl.when(source)
            def _():
                def fetch(i):
                    zz = farthest(i)
                    z_arrival(k, zz).wait_recv()
                    bring(zb_a.at[k, zz], i)

                def arrived(i):
                    zz = farthest(i)
                    pltpu.make_async_copy(zb_a.at[k, zz], stage.at[i], s.st_sem.at[i]).wait()

                loop(Z - 1, fetch)
                loop(Z - 1, arrived)
                total = wide(plane[k, z])
                for i in range(Z - 1):
                    total = total + wide(stage[i])
                plane[k, z] = low(total)
                f_copy(k).start()

        def finish(k):
            @pl.when(source)
            def _():
                f_copy(k).wait_recv()

                @pl.when(k >= 2)
                def _():
                    o_keep(k - 2).wait()
                    o_give(k - 2).wait_send()

                slot = k % 2

                def assemble(first, second):
                    fin[slot, :give_out] = first[:give_out]
                    fin[slot, give_out:wide_out] = low(
                        wide(first[give_out:]) + wide(second[: wide_out - give_out])
                    )
                    fin[slot, wide_out:] = second[wide_out - give_out :]

                @pl.when(xi == 0)
                def _():
                    assemble(plane[k, z], fx[k])

                @pl.when(xi == 1)
                def _():
                    assemble(fx[k], plane[k, z])

                deepen(fin.at[slot], k)
                o_keep(k).start()
                o_give(k).start()

        def vec_copy(i):
            target_r, target_g = here.flip_rep(0)
            for b in range(1, rep_bits):
                other = here.flip_rep(b)
                target_r = jnp.where(i == b, other[0], target_r)
                target_g = jnp.where(i == b, other[1], target_g)
            for b in range(grp_bits):
                other = here.flip_grp(b)
                target_r = jnp.where(i == rep_bits + b, other[0], target_r)
                target_g = jnp.where(i == rep_bits + b, other[1], target_g)
            return remote(
                vec_buf.at[i], vec_got.at[i], s.v_send.at[i], s.v_recv.at[i], (target_r, target_g)
            )

        def swap_all():
            for k in range(1, N):
                loop(Z, lambda zz, k=k: dy_swap(k, zz).start())

        def last_norm():
            back_hidden = dot_tn(w_io[pl.ds(0, 3 * D), :], projT[: 3 * D])
            pull_io(tok_ref, 5).wait()
            normed, inverse = statistics(ioT[...])
            vecT[:, 0:1] = total_of(back_hidden * normed)
            vecT[:, 1:2] = total_of(back_hidden)
            accP[...] = brT[...] + norm_back(back_hidden, normed, inverse, column(0))
            tg_copy.start()
            spread = vecT[:, 12:13]
            for j in range(Q):
                vecT[:, 8 + j : 9 + j] = jnp.where(q == j, spread, 0.0)
            vec_buf[0] = vecT[...].T[:16]
            vec_copy(0).start()

        tg_copy = pltpu.make_async_copy(accP, tg_out, local.at[1])
        bo_copy = pltpu.make_async_copy(resT, bo_out, local.at[0])
        push_vec = pltpu.make_async_copy(vec_own, vec_out, local.at[2])

        def block_done():
            part_to_partner(1, 0).wait_recv()
            part_to_x(1).wait_recv()
            output = resT[...] + wide(prb[1, 0]) + wide(xrb[1])
            resT[...] = jnp.where(live[...] > 0.5, output, 0.0)
            bo_copy.start()

        def vec_round(t):
            vec_copy(t).wait_recv()
            vec_buf[t + 1] = vec_buf[t] + vec_got[t]

            @pl.when(t + 1 < rounds)
            def _():
                vec_copy(t + 1).start()

            @pl.when(t + 1 == rounds)
            def _():
                vecT[:, :16] = vec_buf[rounds].T
                vec_own[...] = vecT[pl.ds(pl.multiple_of(n * g, 8), n), :].T[:16]
                push_vec.start()

        def bring_piece(j):
            return pltpu.make_async_copy(grad_out.at[piece(1, j)], con_in.at[j % 2], s.k_sem.at[2 * G + j % 2])

        def put_block(j, gg):
            return pltpu.make_async_copy(
                con_turn.at[j % 2, rows(n * gg, 0, n), :],
                con_cut.at[rows(Q * n * gg, n * j, n), :],
                s.k_sem.at[G * (j % 2) + gg],
            )

        def con_finals():
            final_keep(1).wait()
            final_arrival(1, 0).wait_recv()
            final_arrival(1, 2).wait_recv()
            bring_piece(0).start()
            bring_piece(1).start()

        def con_piece(j):
            bring_piece(j).wait()

            @pl.when(j >= 2)
            def _():
                loop(G, lambda gg: put_block(j - 2, gg).wait())

            con_turn[j % 2, :D] = con_in[j % 2].T

            @pl.when(j + 2 < Q)
            def _():
                bring_piece(j + 2).start()

            loop(G, lambda gg: put_block(j, gg).start())

        half_size = FF // 2

        def bring_side(half):
            return pltpu.make_async_copy(
                con_cut.at[rows(half_size * half, 0, half_size), :], con_tall, s.k_sem.at[2 * G + 2]
            )

        def put_side(half):
            to = pl.ds(pl.multiple_of(half_size * half, 128), half_size)
            return pltpu.make_async_copy(con_flat, con_out.at[:, to], s.k_sem.at[2 * G + 3])

        def con_side(i):
            @pl.when(i == 0)
            def _():
                loop(G, lambda gg: put_block(Q - 2, gg).wait())
                loop(G, lambda gg: put_block(Q - 1, gg).wait())
                bring_side(0).start()

            @pl.when(i > 0)
            def _():
                half = i - 1
                bring_side(half).wait()

                @pl.when(half == 1)
                def _():
                    put_side(0).wait()

                con_flat[...] = con_tall[...].T
                put_side(half).start()

                @pl.when(half == 0)
                def _():
                    bring_side(1).start()

        served = {11: [(ffn_reduce_y, 0, 0)]}
        steps = [(multiply, 0)]
        for h in range(H):
            steps += [(head_backward, h)] + served.get(h, [])
        steps += [(swap_all,), (multiply, 1), (ffn_reduce_y, 0, 1), (after_x, 0), (multiply, 2), (multiply, 3)]
        steps += [(after_x, 1), (ffn_reduce_y, 0, 2), (last_norm,), (ffn_reduce_y, 0, 3), (after_x, 2), (after_y, 0)]
        steps += [(ffn_reduce_own, 1), (vec_round, 0), (after_x, 3), (after_z, 0), (vec_round, 1)]
        steps += [(after_y, 1), (finish, 0), (vec_round, 2), (block_done,), (ffn_reduce_far, 1), (ffn_reduce_own, 0)]
        steps += [(after_y, 2), (after_z, 1), (vec_round, 3), (con_finals,), (finish, 1), (con_piece, 0)]
        steps += [(after_y, 3), (con_piece, 1), (after_z, 2), (con_piece, 2), (con_piece, 3)]
        steps += [(after_z, 3), (vec_round, 4), (con_side, 0), (finish, 2)]
        steps += [(con_side, 1), (con_side, 2), (ffn_reduce_far, 0), (finish, 3)]
        steps += [(vec_round, t) for t in range(5, rounds)]
        schedule(steps)

        def settle(k):
            @pl.when(source)
            def _():
                @pl.when(z < Z - 1)
                def _():
                    own_copy(k, 0).wait_send()

                @pl.when(z > 0)
                def _():
                    own_copy(k, 1).wait_send()

                own_copy(k, 2).wait_send()

            def each(zz):
                @pl.when((y != c) | (zz != z))
                def _():
                    over_x(k, zz).wait_send()
                    plane_to_partner(k, zz, c).wait_send()
                    rest_to_partner(k, zz, c).wait_send()

                @pl.when(source & (zz != z))
                def _():
                    over_y(k, zz, y).wait_send()

                    @pl.when(goes_on(zz))
                    def _():
                        passing(k, zz).wait_send()

                x_copy(k, zz).wait_send()
                dy_swap(k, zz).wait_send()

                @pl.when(y != c)
                def _():
                    y_copy(k, zz).wait_send()

                @pl.when(source & (zz != z))
                def _():
                    z_copy(k, zz).wait_send()

            loop(Z, each)

            @pl.when(source)
            def _():
                f_copy(k).wait_send()

                @pl.when(k >= N - 2)
                def _():
                    o_keep(k).wait()
                    o_give(k).wait_send()

            @pl.when(y != c)
            def _():
                o_give(k).wait_recv()

        loop(N, settle)

        def settle_ffn(mt):
            @pl.when(z < Z - 1)
            def _():
                ffn_own(mt, 0).wait_send()
                edge_own(mt, 0).wait_send()

            @pl.when(z > 0)
            def _():
                ffn_own(mt, 1).wait_send()
                edge_own(mt, 1).wait_send()


            ffn_own_y(mt).wait_send()

            def each(zz):
                fy_copy(mt, zz).wait_send()

                @pl.when(zz != z)
                def _():
                    ffn_over_y(mt, zz, y).wait_send()

                    @pl.when(goes_on(zz))
                    def _():
                        ffn_pass(mt, zz).wait_send()
                        edge_pass(mt, zz).wait_send()

                @pl.when(zz != z)
                def _():
                    fz_copy(mt, zz).wait_send()

            loop(Z, each)

        for mt in range(2):
            settle_ffn(mt)
            for kind in range(3):
                final_copy(mt, kind).wait_send()
        final_keep(0).wait()
        put_side(1).wait()
        final_arrival(0, 0).wait_recv()
        final_arrival(0, 2).wait_recv()
        for e, buf in ((0, st4), (1, h24)):
            for kind in range(3):
                share_copy(e, buf, kind).wait_send()
        for i in range(2):
            swap_copy(i).wait_send()
        for j in range(2):
            part_to_partner(1, j).wait_send()
        part_to_x(1).wait_send()
        for bit in range(grp_bits):
            small_copy(bit, True).wait_send()
        loop(rounds, lambda i: vec_copy(i).wait_send())
        bo_copy.wait()
        tg_copy.wait()
        push_vec.wait()

    pl.run_scoped(
        closing,
        pltpu.VMEM((N, Z, wide_out, D), BF16),
        pltpu.VMEM((N, Z, give_out, D), BF16),
        pltpu.VMEM((Z, wide_out, D), BF16),
        pltpu.VMEM((2, n, D), BF16),
        pltpu.VMEM((2, n, D), BF16),
        pltpu.VMEM((2, D + PAD, n), BF16),
        pltpu.VMEM((FF // 2, n), BF16),
        pltpu.VMEM((n, FF // 2), BF16),
        pltpu.VMEM((16, n), F32),
    )


def run_layer(lengths, tokens, cotangent, a_in, a_out, w_exp, w_con, vectors, R, G):
    D, T = tokens.shape
    FF = w_con.shape[1]
    n = D // G
    H = D // HD
    Z = G // YSIZE
    Q = TEAM
    N = 4
    give_in = (6 * n // 17) // 8 * 8
    give_out = (5 * n // 17) // 8 * 8
    wide_out = n - give_out
    rounds = bits_of(R) + bits_of(G)
    deep = bits_of(R) - 2
    dma = pltpu.SemaphoreType.DMA
    v = pltpu.VMEM
    scratch = dict(
        w_io=v((4 * D + PAD, D), BF16),
        w_ffn=v((2, D + PAD, D), BF16),
        small_all=v((D + PAD, 128), BF16),
        ioT=v((D, T), F32),
        xo=v((2, D, T), BF16),
        xp=v((2, D, T), BF16),
        projT=v((4 * D + PAD, T), BF16),
        resT=v((D, T), F32),
        h24=v((Q, D, T), BF16),
        st4=v((Q, D, T), BF16),
        brT=v((D, T), F32),
        dyp=v((N, Z, n, T), BF16),
        ps=v((2, D, T), BF16),
        pS=v((D, T), BF16),
        prb=v((2, 2, D, T), BF16),
        xrb=v((2, D, T), BF16),
        accP=v((D, T), F32),
        lse=v((H, 1, T), F32),
        maskb=v((T, T), F32),
        live=v((1, T), F32),
        vecT=v((D, 128), F32),
        vec_buf=v((rounds + 1, 16, D), F32),
        vec_got=v((rounds, 16, D), F32),
        gk=v((2, Z, n, D), BF16),
        gs=v((2, Z, n, D), BF16),
        yb_f=v((2, Z, n, D), BF16),
        zb_f=v((2, Z, n, D), BF16),
        xb=v((N, Z, give_out, D), BF16),
        fx=v((N, wide_out, D), BF16),
        d_tmp=v((n, D) if deep > 0 else (8, 128), BF16),
        l_sem=dma((6,)),
        k_sem=dma((2 * G + 4,)),
        a_own=dma((N, 3)),
        w_own=dma((2, 3)),
        e_send=dma((2, 3)),
        e_recv=dma((2, 3)),
        p_send=dma((2,)),
        p_recv=dma((2,)),
        r_send=dma((2, 3)),
        r_recv=dma((2, 3)),
        s_send=dma((bits_of(G),)),
        s_recv=dma((bits_of(G),)),
        v_send=dma((rounds,)),
        v_recv=dma((rounds,)),
        fo_send=dma((2, 3)),
        fo_recv=dma((2, 3)),
        fo_keep=dma((2,)),
        fz_recv=dma((2, Z)),
        gz_recv=dma((N, Z)),
        gf_send=dma((N,)),
        gf_recv=dma((N,)),
        go_keep=dma((N,)),
        go_send=dma((N,)),
        go_recv=dma((N,)),
        st_sem=dma((Z,)),
        d_send=dma,
        d_local=dma,
        d_recv=dma((N + 2 * Q, max(deep, 1))),
        u_own=dma((2, 2)),
        u_rz=dma((2, Z)),
        u_fwd=dma((2, Z)),
        w_rz=dma((2, Z)),
        w_ry=dma((2, Z)),
        w_fwd=dma((2, Z)),
        w_y=dma((2, Z)),
        fy_send=dma((2, Z)),
        fy_recv=dma((2, Z)),
        fz_send=dma((2, Z)),
        a_rp=dma((N, Z)),
        a_rx=dma((N, Z)),
        a_rcp=dma((N, Z)),
        a_rcx=dma((N, Z)),
        a_fwd=dma((N, Z)),
        a_y=dma((N, Z)),
        a_x=dma((N, Z)),
        a_cp=dma((N, Z)),
        a_cx=dma((N, Z)),
        gx_send=dma((N, Z)),
        gx_recv=dma((N, Z)),
        gy_send=dma((N, Z)),
        gy_recv=dma((N, Z)),
        gz_send=dma((N, Z)),
        dy_send=dma((N, Z)),
        dy_recv=dma((N, Z)),
    )
    hbm = pl.BlockSpec(memory_space=pl.ANY)
    outs = pl.pallas_call(
        functools.partial(layer_kernel, R, G, give_in, give_out, tuple(scratch)),
        out_shape=(
            jax.ShapeDtypeStruct((D, T), F32),
            jax.ShapeDtypeStruct((D, T), F32),
            jax.ShapeDtypeStruct((N + 2 * Q, n, D), BF16),
            jax.ShapeDtypeStruct((n, FF), BF16),
            jax.ShapeDtypeStruct((16, n), F32),
            jax.ShapeDtypeStruct((FF, n), BF16),
            jax.ShapeDtypeStruct((N, Z, wide_out, D), BF16),
            jax.ShapeDtypeStruct((N, Z, wide_out, D), BF16),
            jax.ShapeDtypeStruct((N + 2 * Q, deep, n, D) if deep > 0 else (1, 1, 8, 128), BF16),
        ),
        in_specs=[pl.BlockSpec(memory_space=pltpu.SMEM)] + [hbm] * 6 + [pl.BlockSpec(memory_space=pltpu.VMEM)] * 9,
        out_specs=(hbm,) * 9,
        scratch_shapes=list(scratch.values()),
        compiler_params=pltpu.CompilerParams(collective_id=0, has_side_effects=True, vmem_limit_bytes=VMEM_LIMIT),
        name="layer",
    )(lengths, tokens, cotangent, a_in, a_out, w_exp, w_con, *vectors)
    return outs[:5]


def per_device(
    tokens,
    document_lengths,
    cotangent,
    first_gain,
    first_shift,
    attention_in,
    query_bias,
    value_bias,
    attention_out,
    output_bias,
    second_gain,
    second_shift,
    expand_weight,
    expand_bias,
    contract_weight,
    contract_bias,
):
    R, G = lax.axis_size("rep"), lax.axis_size("grp")
    T, D = tokens.shape
    n = D // G
    Q = TEAM
    vectors = [
        first_gain,
        first_shift,
        query_bias,
        value_bias,
        output_bias,
        second_gain,
        second_shift,
        contract_bias,
        expand_bias,
    ]
    block_t, tokens_t, grads, con_grad, share = run_layer(
        document_lengths,
        tokens.T,
        cotangent.T,
        attention_in.T,
        attention_out.T,
        expand_weight.T,
        contract_weight.T,
        vectors,
        R,
        G,
    )
    out_grad = grads[0].T.astype(F32)
    in_grad = grads[1:4].reshape(3 * n, D).T.astype(F32)
    exp_grad = grads[4 : 4 + Q].reshape(Q * n, D).T.astype(F32)
    con_grad = con_grad.T.astype(F32)
    return (
        block_t.T,
        tokens_t.T,
        share[0],
        share[1],
        in_grad,
        share[2],
        share[3],
        out_grad,
        share[4],
        share[5],
        share[6],
        exp_grad,
        share[8 : 8 + Q].reshape(Q * n),
        con_grad,
        share[7],
    )


def solution(mesh):
    rows = P(("rep", "grp"), None)
    split, columns = P("grp"), P(None, "grp")
    return jax.shard_map(
        per_device,
        mesh=mesh,
        in_specs=(
            rows,
            rows,
            rows,
            split,
            split,
            columns,
            split,
            split,
            columns,
            split,
            split,
            split,
            columns,
            split,
            columns,
            split,
        ),
        out_specs=(
            rows,
            rows,
            split,
            split,
            columns,
            split,
            split,
            columns,
            split,
            split,
            split,
            columns,
            split,
            columns,
            split,
        ),
        check_vma=False,
    )
```

time: 1770 us -> 242 us (0.14)
  waiting for transfers between devices: 1520 us -> 0 us
  Pallas kernels: 0 us -> 225 us
  blocking collectives: 92.8 us -> 0 us
  matrix products: 71.6 us -> 0 us
  local copies, waits for them, and re-layouts: 64.8 us -> 8.34 us
    reduce_scatter x2 -> x0, waiting for transfers between devices: 854 us -> none  [the longest x1 473 us: per_device(): lax.psum_scatter(blocks[2], ('rep', 'grp'), scatter_dimension=0, tiled=True)]
    all_gather x7 -> x0, waiting for transfers between devices: 439 us -> none  [the longest x1 137 us: per_device(): lax.all_gather(expand_weight, 'grp', axis=1, tiled=True)]
    pallas_call x0 -> x1, Pallas kernels: none -> 225 us  [run_layer(): pl.pallas_call(functools.partial(layer_kernel, R, G, give_in, give_out, t...]
    unnamed x13 -> x0, waiting for transfers between devices: 221 us -> none
    dot_general x18 -> x0, matrix products: 71.6 us -> none  [the longest x8 52.2 us: matmul(): return jnp.dot(left, right, preferred_element_type=jnp.float32)]
    unnamed x1 -> x0, blocking collectives: 42.2 us -> none
    psum x1 -> x0, blocking collectives: 41.4 us -> none  [per_device(): lax.psum((vectors[0], vectors[1], vectors[2], vectors[3], vectors[4], vec...]
    transpose x4 -> x0, local copies, waits for them, and re-layouts: 27.1 us -> none  [split_both(): jnp.einsum('tri,tgj->rgij', left_blocks, right_blocks, preferred_element_...]
  transfers between devices with their start and end apart: 11 -> 0, of which waited for: 11 -> 0; matrix products, arithmetic and copies ran while one was open for 6% -> 0% of each run, Pallas kernels for 0% -> 0%
where the time goes in v2:
time: 242 us; the launch traced here: 241 us
  Pallas kernels  225 us (93%)
  local copies, waits for them, and re-layouts  8.34 us (3%)
  other arithmetic  6.56 us (3%)
    pallas_call x1, Pallas kernels, run_layer(): pl.pallas_call(functools.partial(layer_kernel, R, G, give_in, give_out, t...  225 us

profile of v2, /device:TPU:0, one launch (start us, length us, event | category | flops | bytes accessed | tf_op | source)
XLA Modules:
  0.0 240.5 jit_solution(8993931219799207056)
XLA Ops:
  0.7 225.0 %layer.1 = (f32[1088,256]{1,0:T(8,128)}, f32[1088,256]{1,0:T(8,128)}, bf16[12,136,1088]{2,1,0:T(8,128)(2,1)}, bf16[136,4352]{1,0:T(8,128)(2,1)}, f32[16,136]{1,0...) custom-call(s32[1,8]{1,0:T(1,128)} %refs_0_.1, ...), custom_call_target="tpu_custom_call" | custom-call | tf_op jit(solution)/shard_map/layer/pallas_call | solution.py:1395
  225.6 0.7 slice.46
  226.3 1.6 fusion
  227.9 0.7 reshape.41
  228.6 1.8 convert_bitcast_fusion.3
  230.4 1.3 slice.38
  231.7 1.4 slice.45
  233.1 1.4 convert_bitcast_fusion.2
  234.5 0.0 copy-start
  234.5 1.7 convert_bitcast_fusion
  236.2 0.0 copy-done
  236.2 0.0 copy-start.2
  236.2 1.6 convert_bitcast_fusion.1
  237.8 0.1 copy-done.2
  237.9 0.0 copy-start.1
  237.9 1.0 copy.33
  238.9 0.7 copy-done.1
  239.5 1.0 copy.34
Async XLA Ops:
  234.5 1.7 copy-start
  236.2 1.7 copy-start.2
  237.9 1.6 copy-start.1

commit v3 on v2

--- a/solution.py
+++ b/solution.py
@@ -111,8 +111,9 @@
 def layer_kernel(R, G, give_in, give_out, names, *refs):
     len_ref, tok_ref, cot_ref, ain_ref, aout_ref, exp_ref, con_ref = refs[:7]
     vector_refs = refs[7:16]
-    bo_out, tg_out, grad_out, con_out, vec_out, con_cut, yb_a, zb_a, deep_buf = refs[16:25]
-    s = types.SimpleNamespace(**dict(zip(names, refs[25:])))
+    bo_out, tg_out, in_out, out_out, exp_out, con_out, vec_out, con_raw, con_cut, yb_a, zb_a, deep_buf = refs[16:28]
+    s = types.SimpleNamespace(**dict(zip(names, refs[28:])))
+    ffn_out = (exp_out, con_raw)
     here = Place(R, G)
     Z, z, y, c, xi, q, g = here.Z, here.z, here.y, here.c, here.xi, here.q, here.g
     D, T = tok_ref.shape
@@ -168,6 +169,19 @@
                 pick = jnp.where((z == at) & (i == j), table[at][j], pick)
         return pick
 
+    assert Z == 4
+    at_end = (z == 0) | (z == Z - 1)
+    mate = z + 1 - 2 * (z % 2)
+
+    def is_far(zz):
+        return (zz != z) & (zz != mate)
+
+    def line_target(zz):
+        return here.on_line(jnp.where((zz == mate) | at_end, mate, zz))
+
+    def line_slot(zz):
+        return jnp.where(zz == mate, z, zz)
+
     def goes_on(zz):
         return ((zz < z) & (z < Z - 1)) | ((zz > z) & (z > 0))
 
@@ -399,14 +413,11 @@
         return remote(gs.at[mt, zz], yb_f.at[mt, zz], s.fy_send.at[mt, zz], s.fy_recv.at[mt, zz], here.ynbr)
 
     def fz_copy(mt, zz):
-        return remote(
-            gk.at[mt, zz], zb_f.at[mt, z], s.fz_send.at[mt, zz], s.fz_recv.at[mt, z], here.on_line(zz)
-        )
-
-    def fz_arrival(mt, zz):
-        return remote(
-            gk.at[mt, zz], zb_f.at[mt, zz], s.fz_send.at[mt, zz], s.fz_recv.at[mt, zz], here.on_line(zz)
-        )
+        slot = line_slot(zz)
+        return remote(gk.at[mt, zz], zb_f.at[mt, slot], s.fz_send.at[mt, zz], s.fz_recv.at[mt, slot], line_target(zz))
+
+    def fz_arrival(mt, slot):
+        return remote(gk.at[mt, slot], zb_f.at[mt, slot], s.fz_send.at[mt, slot], s.fz_recv.at[mt, slot], line_target(mate))
 
     def piece(mt, which):
         return N + Q * mt + which
@@ -414,18 +425,18 @@
     def final_copy(mt, kind):
         target = (here.partner, here.xnbr, here.partner)[kind]
         slot = (q, q, here.q_x)[kind]
-        src = grad_out.at[piece(mt, slot)] if kind == 2 else gk.at[mt, z]
-        dst = grad_out.at[piece(mt, slot)]
+        src = ffn_out[mt].at[slot] if kind == 2 else gk.at[mt, z]
+        dst = ffn_out[mt].at[slot]
         return remote(src, dst, s.fo_send.at[mt, kind], s.fo_recv.at[mt, kind], target)
 
     def final_arrival(mt, kind):
         target = (here.partner, here.xnbr, here.partner)[kind]
         slot = (here.q_partner, here.q_x, here.q_far)[kind]
-        ref = grad_out.at[piece(mt, slot)]
+        ref = ffn_out[mt].at[slot]
         return remote(ref, ref, s.fo_send.at[mt, kind], s.fo_recv.at[mt, kind], target)
 
     def final_keep(mt):
-        return pltpu.make_async_copy(gk.at[mt, z], grad_out.at[piece(mt, q)], s.fo_keep.at[mt])
+        return pltpu.make_async_copy(gk.at[mt, z], ffn_out[mt].at[q], s.fo_keep.at[mt])
 
     def deepen(ref, k):
         for bit in range(2, rep_bits):
@@ -464,25 +475,43 @@
         fy_copy(mt, zz).wait_recv()
         gk[mt, zz] = low(wide(gk[mt, zz]) + wide(yb_f[mt, zz]))
 
-        @pl.when(zz != z)
+        @pl.when((zz == mate) | (at_end & (zz != z)))
         def _():
             fz_copy(mt, zz).start()
 
+    def ffn_relay(mt):
+        def each(i):
+            zz = farthest(i)
+
+            @pl.when(is_far(zz) & jnp.logical_not(at_end))
+            def _():
+                fz_arrival(mt, zz).wait_recv()
+                gk[mt, zz] = low(wide(gk[mt, zz]) + wide(zb_f[mt, zz]))
+                fz_copy(mt, zz).start()
+
+        loop(Z, each)
+
     def ffn_reduce_own(mt):
-        total = wide(gk[mt, z])
-        for i in range(Z - 1):
-            zz = farthest(i)
-            fz_arrival(mt, zz).wait_recv()
-            total = total + wide(zb_f[mt, zz])
+        fz_arrival(mt, mate).wait_recv()
+        fz_arrival(mt, z).wait_recv()
+        total = wide(gk[mt, z]) + wide(zb_f[mt, mate]) + wide(zb_f[mt, z])
         gk[mt, z] = low(total)
         deepen(gk.at[mt, z], piece(mt, 0))
-        final_keep(mt).start()
-        final_copy(mt, 0).start()
-        final_copy(mt, 1).start()
+        for m in range(2):
+
+            @pl.when(mt == m)
+            def _(m=m):
+                final_keep(m).start()
+                final_copy(m, 0).start()
+                final_copy(m, 1).start()
 
     def ffn_reduce_far(mt):
-        final_arrival(mt, 1).wait_recv()
-        final_copy(mt, 2).start()
+        for m in range(2):
+
+            @pl.when(mt == m)
+            def _(m=m):
+                final_arrival(m, 1).wait_recv()
+                final_copy(m, 2).start()
 
     def column(j, at=None):
         block = small_all[: D] if at is None else small_all[at, :]
@@ -527,6 +556,22 @@
                     act(*picked)
 
         loop(len(steps), body)
+
+    def ranges(head, served):
+        def run(first, last):
+            def each(h, carry):
+                head(h)
+                return carry
+
+            lax.fori_loop(first, last, each, 0)
+
+        steps, first = [], 0
+        for h in sorted(served):
+            steps += [(run, first, h + 1)] + served[h]
+            first = h + 1
+        if first < H:
+            steps += [(run, first, H)]
+        return steps
 
     local = s.l_sem
 
@@ -666,15 +711,12 @@
         steps += [(project,), (ffn_edges, 0, 0), (gather_wave, 4, 1), (share_start,)]
         served = {
             2: [(ffn_wave, 0, 2)],
-            5: [(ffn_edges, 0, 1)],
-            8: [(start_ffn, 1)],
-            10: [(ffn_edges, 0, 2)],
-            13: [(ffn_wave, 0, 3), (start_ffn_y, 1)],
-            15: [(ffn_edges, 0, 3)],
+            6: [(ffn_edges, 0, 1), (start_ffn, 1)],
+            11: [(ffn_wave, 0, 3), (start_ffn_y, 1)],
+            14: [(ffn_edges, 0, 2)],
             16: [(pass_start,)],
         }
-        for h in range(H):
-            steps += [(head_forward, h)] + served.get(h, [])
+        steps += ranges(head_forward, served)
         schedule(steps)
 
     pl.run_scoped(
@@ -814,7 +856,7 @@
             def _():
                 gp4[0] = brT[...]
 
-        steps = [(ffn_wave, 1, 1), (ffn_y_arrivals, 0), (expand_step, 0), (ffn_wave, 1, 2), (expand_step, 1)]
+        steps = [(ffn_edges, 0, 3), (ffn_wave, 1, 1), (ffn_y_arrivals, 0), (expand_step, 0), (ffn_wave, 1, 2), (expand_step, 1)]
         steps += [(ffn_edges, 1, 0), (ffn_wave, 1, 3), (expand_step, 2), (ffn_edges, 1, 1), (expand_step, 3)]
         steps += [(ffn_edges, 1, 2), (gradients,), (ffn_edges, 1, 3), (ffn_y_arrivals, 1)]
         steps += [(back_step, 0), (back_step, 1), (ffn_reduce_y, 1, 0), (back_step, 2), (ffn_reduce_y, 1, 1)]
@@ -876,23 +918,26 @@
             return remote(plane.at[k, zz], yb_a.at[k, zz], s.gy_send.at[k, zz], s.gy_recv.at[k, zz], here.ynbr)
 
         def z_copy(k, zz):
+            slot = line_slot(zz)
             return remote(
-                plane.at[k, zz], zb_a.at[k, z], s.gz_send.at[k, zz], s.gz_recv.at[k, z], here.on_line(zz)
+                plane.at[k, zz], zb_a.at[k, slot], s.gz_send.at[k, zz], s.gz_recv.at[k, slot], line_target(zz)
             )
 
-        def z_arrival(k, zz):
+        def z_arrival(k, slot):
             return remote(
-                plane.at[k, zz], zb_a.at[k, zz], s.gz_send.at[k, zz], s.gz_recv.at[k, zz], here.on_line(zz)
+                plane.at[k, slot], zb_a.at[k, slot], s.gz_send.at[k, slot], s.gz_recv.at[k, slot], line_target(mate)
             )
 
         def f_copy(k):
             return remote(plane.at[k, z], fx.at[k], s.gf_send.at[k], s.gf_recv.at[k], here.xnbr)
 
-        def o_keep(k):
-            return pltpu.make_async_copy(fin.at[k % 2], grad_out.at[k], s.go_keep.at[k])
-
-        def o_give(k):
-            return remote(fin.at[k % 2], grad_out.at[k], s.go_send.at[k], s.go_recv.at[k], here.partner)
+        def o_keep(k, dst):
+            return pltpu.make_async_copy(fin.at[k % 2], dst, s.go_keep.at[k])
+
+        def o_give(k, dst):
+            return remote(fin.at[k % 2], dst, s.go_send.at[k], s.go_recv.at[k], here.partner)
+
+        any_out = in_out.at[0]
 
         def bring(src, slot):
             copy = pltpu.make_async_copy(src, stage.at[slot], s.st_sem.at[slot])
@@ -961,7 +1006,7 @@
                     pltpu.make_async_copy(yb_a.at[k, zz], stage.at[i], s.st_sem.at[i]).wait()
                     plane[k, zz] = low(wide(plane[k, zz]) + wide(stage[i]))
 
-                    @pl.when(i < Z - 1)
+                    @pl.when((zz == mate) | (at_end & (zz != z)))
                     def _():
                         z_copy(k, zz).start()
 
@@ -976,24 +1021,29 @@
 
                 loop(Z + 1, step)
 
+        def relay(k):
+            def each(i):
+                zz = farthest(i)
+
+                @pl.when(source & is_far(zz) & jnp.logical_not(at_end))
+                def _():
+                    z_arrival(k, zz).wait_recv()
+                    bring(zb_a.at[k, zz], i).wait()
+                    plane[k, zz] = low(wide(plane[k, zz]) + wide(stage[i]))
+                    z_copy(k, zz).start()
+
+            loop(Z, each)
+
         def after_z(k):
             @pl.when(source)
             def _():
-                def fetch(i):
-                    zz = farthest(i)
-                    z_arrival(k, zz).wait_recv()
-                    bring(zb_a.at[k, zz], i)
-
-                def arrived(i):
-                    zz = farthest(i)
-                    pltpu.make_async_copy(zb_a.at[k, zz], stage.at[i], s.st_sem.at[i]).wait()
-
-                loop(Z - 1, fetch)
-                loop(Z - 1, arrived)
-                total = wide(plane[k, z])
-                for i in range(Z - 1):
-                    total = total + wide(stage[i])
-                plane[k, z] = low(total)
+                z_arrival(k, mate).wait_recv()
+                near = bring(zb_a.at[k, mate], 0)
+                z_arrival(k, z).wait_recv()
+                far = bring(zb_a.at[k, z], 1)
+                near.wait()
+                far.wait()
+                plane[k, z] = low(wide(plane[k, z]) + wide(stage[0]) + wide(stage[1]))
                 f_copy(k).start()
 
         def finish(k):
@@ -1003,8 +1053,8 @@
 
                 @pl.when(k >= 2)
                 def _():
-                    o_keep(k - 2).wait()
-                    o_give(k - 2).wait_send()
+                    o_keep(k - 2, any_out).wait()
+                    o_give(k - 2, any_out).wait_send()
 
                 slot = k % 2
 
@@ -1024,8 +1074,16 @@
                     assemble(fx[k], plane[k, z])
 
                 deepen(fin.at[slot], k)
-                o_keep(k).start()
-                o_give(k).start()
+                @pl.when(k == 0)
+                def _():
+                    o_keep(k, out_out).start()
+                    o_give(k, out_out).start()
+
+                @pl.when(k > 0)
+                def _():
+                    o_keep(k, in_out.at[k - 1]).start()
+                    o_give(k, in_out.at[k - 1]).start()
+
 
         def vec_copy(i):
             target_r, target_g = here.flip_rep(0)
@@ -1085,7 +1143,7 @@
                 push_vec.start()
 
         def bring_piece(j):
-            return pltpu.make_async_copy(grad_out.at[piece(1, j)], con_in.at[j % 2], s.k_sem.at[2 * G + j % 2])
+            return pltpu.make_async_copy(con_raw.at[j], con_in.at[j % 2], s.k_sem.at[2 * G + j % 2])
 
         def put_block(j, gg):
             return pltpu.make_async_copy(
@@ -1150,18 +1208,16 @@
                 def _():
                     bring_side(1).start()
 
-        served = {11: [(ffn_reduce_y, 0, 0)]}
-        steps = [(multiply, 0)]
-        for h in range(H):
-            steps += [(head_backward, h)] + served.get(h, [])
-        steps += [(swap_all,), (multiply, 1), (ffn_reduce_y, 0, 1), (after_x, 0), (multiply, 2), (multiply, 3)]
-        steps += [(after_x, 1), (ffn_reduce_y, 0, 2), (last_norm,), (ffn_reduce_y, 0, 3), (after_x, 2), (after_y, 0)]
-        steps += [(ffn_reduce_own, 1), (vec_round, 0), (after_x, 3), (after_z, 0), (vec_round, 1)]
-        steps += [(after_y, 1), (finish, 0), (vec_round, 2), (block_done,), (ffn_reduce_far, 1), (ffn_reduce_own, 0)]
-        steps += [(after_y, 2), (after_z, 1), (vec_round, 3), (con_finals,), (finish, 1), (con_piece, 0)]
-        steps += [(after_y, 3), (con_piece, 1), (after_z, 2), (con_piece, 2), (con_piece, 3)]
-        steps += [(after_z, 3), (vec_round, 4), (con_side, 0), (finish, 2)]
-        steps += [(con_side, 1), (con_side, 2), (ffn_reduce_far, 0), (finish, 3)]
+        served = {7: [(ffn_relay, 1)], 13: [(ffn_reduce_y, 0, 0)]}
+        steps = [(multiply, 0)] + ranges(head_backward, served)
+        steps += [(swap_all,), (last_norm,), (multiply, 1), (ffn_reduce_y, 0, 1), (vec_round, 0), (after_x, 0)]
+        steps += [(multiply, 2), (multiply, 3), (ffn_reduce_y, 0, 2), (ffn_reduce_y, 0, 3), (after_x, 1), (vec_round, 1)]
+        steps += [(ffn_reduce_own, 1), (after_x, 2), (after_y, 0), (ffn_relay, 0), (after_x, 3)]
+        steps += [(relay, 0), (after_y, 1), (vec_round, 2), (relay, 1), (after_y, 2), (after_z, 0), (block_done,)]
+        steps += [(relay, 2), (ffn_reduce_far, 1), (after_y, 3), (after_z, 1), (vec_round, 3), (relay, 3)]
+        steps += [(finish, 0), (ffn_reduce_own, 0), (after_z, 2), (con_finals,), (finish, 1), (con_piece, 0)]
+        steps += [(con_piece, 1), (con_piece, 2), (con_piece, 3), (after_z, 3), (con_side, 0), (vec_round, 4)]
+        steps += [(finish, 2), (con_side, 1), (con_side, 2), (ffn_reduce_far, 0), (finish, 3)]
         steps += [(vec_round, t) for t in range(5, rounds)]
         schedule(steps)
 
@@ -1212,12 +1268,12 @@
 
                 @pl.when(k >= N - 2)
                 def _():
-                    o_keep(k).wait()
-                    o_give(k).wait_send()
+                    o_keep(k, any_out).wait()
+                    o_give(k, any_out).wait_send()
 
             @pl.when(y != c)
             def _():
-                o_give(k).wait_recv()
+                o_give(k, any_out).wait_recv()
 
         loop(N, settle)
 
@@ -1299,7 +1355,7 @@
     Q = TEAM
     N = 4
     give_in = (6 * n // 17) // 8 * 8
-    give_out = (5 * n // 17) // 8 * 8
+    give_out = (6 * n // 17) // 8 * 8
     wide_out = n - give_out
     rounds = bits_of(R) + bits_of(G)
     deep = bits_of(R) - 2
@@ -1397,21 +1453,24 @@
         out_shape=(
             jax.ShapeDtypeStruct((D, T), F32),
             jax.ShapeDtypeStruct((D, T), F32),
-            jax.ShapeDtypeStruct((N + 2 * Q, n, D), BF16),
+            jax.ShapeDtypeStruct((3, n, D), BF16),
+            jax.ShapeDtypeStruct((n, D), BF16),
+            jax.ShapeDtypeStruct((Q, n, D), BF16),
             jax.ShapeDtypeStruct((n, FF), BF16),
             jax.ShapeDtypeStruct((16, n), F32),
+            jax.ShapeDtypeStruct((Q, n, D), BF16),
             jax.ShapeDtypeStruct((FF, n), BF16),
             jax.ShapeDtypeStruct((N, Z, wide_out, D), BF16),
             jax.ShapeDtypeStruct((N, Z, wide_out, D), BF16),
             jax.ShapeDtypeStruct((N + 2 * Q, deep, n, D) if deep > 0 else (1, 1, 8, 128), BF16),
         ),
         in_specs=[pl.BlockSpec(memory_space=pltpu.SMEM)] + [hbm] * 6 + [pl.BlockSpec(memory_space=pltpu.VMEM)] * 9,
-        out_specs=(hbm,) * 9,
+        out_specs=(hbm,) * 12,
         scratch_shapes=list(scratch.values()),
         compiler_params=pltpu.CompilerParams(collective_id=0, has_side_effects=True, vmem_limit_bytes=VMEM_LIMIT),
         name="layer",
     )(lengths, tokens, cotangent, a_in, a_out, w_exp, w_con, *vectors)
-    return outs[:5]
+    return outs[:7]
 
 
 def per_device(
@@ -1447,7 +1506,7 @@
         contract_bias,
         expand_bias,
     ]
-    block_t, tokens_t, grads, con_grad, share = run_layer(
+    block_t, tokens_t, in_grad, out_grad, exp_grad, con_grad, share = run_layer(
         document_lengths,
         tokens.T,
         cotangent.T,
@@ -1459,9 +1518,9 @@
         R,
         G,
     )
-    out_grad = grads[0].T.astype(F32)
-    in_grad = grads[1:4].reshape(3 * n, D).T.astype(F32)
-    exp_grad = grads[4 : 4 + Q].reshape(Q * n, D).T.astype(F32)
+    out_grad = out_grad.T.astype(F32)
+    in_grad = in_grad.reshape(3 * n, D).T.astype(F32)
+    exp_grad = exp_grad.reshape(Q * n, D).T.astype(F32)
     con_grad = con_grad.T.astype(F32)
     return (
         block_t.T,

time: 242 us -> 234 us (0.967)
  Pallas kernels: 225 us -> 219 us
    pallas_call x1, Pallas kernels: 225 us -> 219 us  [run_layer(): pl.pallas_call(functools.partial(layer_kernel, R, G, give_in, give_out, t...]
    slice x2 -> x0, local copies, waits for them, and re-layouts: 2.65 us -> none  [the longest x1 1.39 us: per_device(): exp_grad = grads[4:4 + Q].reshape(Q * n, D).T.astype(F32)]
where the time goes in v3:
time: 234 us; the launch traced here: 233 us
  Pallas kernels  219 us (94%)
  other arithmetic  6.55 us (3%)
  local copies, waits for them, and re-layouts  6.13 us (3%)
    pallas_call x1, Pallas kernels, run_layer(): pl.pallas_call(functools.partial(layer_kernel, R, G, give_in, give_out, t...  219 us

profile of v3, /device:TPU:0, one launch (start us, length us, event | category | flops | bytes accessed | tf_op | source)
XLA Modules:
  0.0 232.7 jit_solution(2622835781613320429)
XLA Ops:
  0.7 219.3 %layer.1 = (f32[1088,256]{1,0:T(8,128)}, f32[1088,256]{1,0:T(8,128)}, bf16[3,136,1088]{2,1,0:T(8,128)(2,1)}, bf16[136,1088]{1,0:T(8,128)(2,1)}, bf16[4,136,1088]...) custom-call(s32[1,8]{1,0:T(1,128)} %refs_0_.1, ...), custom_call_target="tpu_custom_call" | custom-call | tf_op jit(solution)/shard_map/layer/pallas_call | solution.py:1451
  220.0 0.0 copy-start.4
  220.0 0.8 slice.34
  220.8 1.6 fusion
  222.4 0.7 reshape.39
  223.0 1.8 convert_bitcast_fusion.3
  224.9 0.0 copy-done.4
  224.9 0.0 copy-start.1
  224.9 1.4 convert_bitcast_fusion.2
  226.3 0.2 copy-done.1
  226.5 0.0 copy-start
  226.5 1.6 convert_bitcast_fusion.1
  228.1 0.3 copy-done
  228.3 0.0 copy-start.3
  228.3 1.7 convert_bitcast_fusion
  230.0 0.0 copy-done.3
  230.0 0.0 copy-start.2
  230.0 1.0 copy.33
  231.0 0.7 copy-done.2
  231.7 1.0 copy.34
Async XLA Ops:
  220.0 4.9 %copy-start.4 = (bf16[3,136,1088]{2,1,0:T(8,128)(2,1)S(1)}, bf16[3,136,1088]{2,1,0:T(8,128)(2,1)}, u32[]{:S(2)}) copy-start(bf16[3,136,1088]{2,1,0:T(8,128)(2,1)} %get-tuple-element.25) | copy-start | bytes 2663428
  224.9 1.6 copy-start.1
  226.5 1.8 copy-start
  228.3 1.7 copy-start.3
  230.0 1.6 copy-start.2

commit v4 on v3

--- a/solution.py
+++ b/solution.py
@@ -409,8 +409,41 @@
         ref = small_all.at[rows(n * base, 0, n * size), :]
         return remote(ref, ref, s.s_send.at[bit], s.s_recv.at[bit], here.flip_grp(bit))
 
+    main = n - first_y
+    main_rows, edge_rows = pl.ds(0, main), pl.ds(main, first_y)
+
     def fy_copy(mt, zz):
-        return remote(gs.at[mt, zz], yb_f.at[mt, zz], s.fy_send.at[mt, zz], s.fy_recv.at[mt, zz], here.ynbr)
+        return remote(
+            gs.at[mt, zz, main_rows],
+            yb_f.at[mt, zz, main_rows],
+            s.fy_send.at[mt, zz],
+            s.fy_recv.at[mt, zz],
+            here.ynbr,
+        )
+
+    def edge_y(mt):
+        return remote(
+            gs.at[mt, z, edge_rows], yb_f.at[mt, z, edge_rows], s.ue_send.at[mt], s.ue_recv.at[mt], here.ynbr
+        )
+
+    def edge_copy(mt, zz):
+        return remote(
+            gs.at[mt, zz, edge_rows], s.zb_e.at[mt, z], s.uz_send.at[mt, zz], s.uz_recv.at[mt, z], here.on_line(zz)
+        )
+
+    def edge_arrival(mt, zz):
+        return remote(
+            gs.at[mt, zz, edge_rows], s.zb_e.at[mt, zz], s.uz_send.at[mt, zz], s.uz_recv.at[mt, zz], here.on_line(zz)
+        )
+
+    def edge_over(mt):
+        total = wide(gs[mt, z, main:])
+        for i in range(Z - 1):
+            zz = farthest(i)
+            edge_arrival(mt, zz).wait_recv()
+            total = total + wide(s.zb_e[mt, zz])
+        gs[mt, z, main:] = low(total)
+        edge_y(mt).start()
 
     def fz_copy(mt, zz):
         slot = line_slot(zz)
@@ -468,12 +501,16 @@
 
             fy_copy(mt, b).start()
 
+            @pl.when(b != z)
+            def _():
+                edge_copy(mt, b).start()
+
         loop(Z, lambda i: block(farthest(i)))
 
     def ffn_reduce_y(mt, i):
         zz = farthest(i)
         fy_copy(mt, zz).wait_recv()
-        gk[mt, zz] = low(wide(gk[mt, zz]) + wide(yb_f[mt, zz]))
+        gk[mt, zz, :main] = low(wide(gk[mt, zz, :main]) + wide(yb_f[mt, zz, :main]))
 
         @pl.when((zz == mate) | (at_end & (zz != z)))
         def _():
@@ -495,7 +532,9 @@
         fz_arrival(mt, mate).wait_recv()
         fz_arrival(mt, z).wait_recv()
         total = wide(gk[mt, z]) + wide(zb_f[mt, mate]) + wide(zb_f[mt, z])
-        gk[mt, z] = low(total)
+        edge_y(mt).wait_recv()
+        gk[mt, z, :main] = low(total[:main])
+        gk[mt, z, main:] = low(total[main:] + wide(yb_f[mt, z, main:]))
         deepen(gk.at[mt, z], piece(mt, 0))
         for m in range(2):
 
@@ -878,7 +917,6 @@
         part_to_x(0).wait_send()
         part_to_partner(1, 1).wait_recv()
         pS[...] = low(gp4[1] + wide(prb[1, 1]))
-        part_to_x(1).start()
         resT[...] = resT[...] + gp4[0] + column(7)
         vecT[:, 4:5] = total_of(brT[...])
 
@@ -1121,6 +1159,9 @@
         bo_copy = pltpu.make_async_copy(resT, bo_out, local.at[0])
         push_vec = pltpu.make_async_copy(vec_own, vec_out, local.at[2])
 
+        def send_out():
+            part_to_x(1).start()
+
         def block_done():
             part_to_partner(1, 0).wait_recv()
             part_to_x(1).wait_recv()
@@ -1208,15 +1249,16 @@
                 def _():
                     bring_side(1).start()
 
-        served = {7: [(ffn_relay, 1)], 13: [(ffn_reduce_y, 0, 0)]}
+        served = {7: [(edge_over, 1), (ffn_relay, 1)], 13: [(edge_over, 0), (ffn_reduce_y, 0, 0)]}
         steps = [(multiply, 0)] + ranges(head_backward, served)
         steps += [(swap_all,), (last_norm,), (multiply, 1), (ffn_reduce_y, 0, 1), (vec_round, 0), (after_x, 0)]
         steps += [(multiply, 2), (multiply, 3), (ffn_reduce_y, 0, 2), (ffn_reduce_y, 0, 3), (after_x, 1), (vec_round, 1)]
+        steps += [(send_out,)]
         steps += [(ffn_reduce_own, 1), (after_x, 2), (after_y, 0), (ffn_relay, 0), (after_x, 3)]
-        steps += [(relay, 0), (after_y, 1), (vec_round, 2), (relay, 1), (after_y, 2), (after_z, 0), (block_done,)]
-        steps += [(relay, 2), (ffn_reduce_far, 1), (after_y, 3), (after_z, 1), (vec_round, 3), (relay, 3)]
-        steps += [(finish, 0), (ffn_reduce_own, 0), (after_z, 2), (con_finals,), (finish, 1), (con_piece, 0)]
-        steps += [(con_piece, 1), (con_piece, 2), (con_piece, 3), (after_z, 3), (con_side, 0), (vec_round, 4)]
+        steps += [(relay, 0), (after_y, 1), (vec_round, 2), (relay, 1), (after_y, 2), (after_z, 0)]
+        steps += [(relay, 2), (after_y, 3), (after_z, 1), (vec_round, 3), (relay, 3)]
+        steps += [(ffn_reduce_far, 1), (finish, 0), (ffn_reduce_own, 0), (after_z, 2), (con_finals,), (finish, 1), (con_piece, 0)]
+        steps += [(con_piece, 1), (con_piece, 2), (con_piece, 3), (block_done,), (after_z, 3), (con_side, 0), (vec_round, 4)]
         steps += [(finish, 2), (con_side, 1), (con_side, 2), (ffn_reduce_far, 0), (finish, 3)]
         steps += [(vec_round, t) for t in range(5, rounds)]
         schedule(steps)
@@ -1290,6 +1332,8 @@
 
 
             ffn_own_y(mt).wait_send()
+
+            edge_y(mt).wait_send()
 
             def each(zz):
                 fy_copy(mt, zz).wait_send()
@@ -1306,6 +1350,7 @@
                 @pl.when(zz != z)
                 def _():
                     fz_copy(mt, zz).wait_send()
+                    edge_copy(mt, zz).wait_send()
 
             loop(Z, each)
 
@@ -1389,6 +1434,7 @@
         gs=v((2, Z, n, D), BF16),
         yb_f=v((2, Z, n, D), BF16),
         zb_f=v((2, Z, n, D), BF16),
+        zb_e=v((2, Z, (3 * n // 17) // 8 * 8, D), BF16),
         xb=v((N, Z, give_out, D), BF16),
         fx=v((N, wide_out, D), BF16),
         d_tmp=v((n, D) if deep > 0 else (8, 128), BF16),
@@ -1421,6 +1467,10 @@
         d_local=dma,
         d_recv=dma((N + 2 * Q, max(deep, 1))),
         u_own=dma((2, 2)),
+        ue_send=dma((2,)),
+        ue_recv=dma((2,)),
+        uz_send=dma((2, Z)),
+        uz_recv=dma((2, Z)),
         u_rz=dma((2, Z)),
         u_fwd=dma((2, Z)),
         w_rz=dma((2, Z)),

time: 234 us -> 233 us (level); the launches traced: 233 us -> 229 us
  Pallas kernels: 219 us -> 216 us
    pallas_call x1, Pallas kernels: 219 us -> 216 us  [run_layer(): pl.pallas_call(functools.partial(layer_kernel, R, G, give_in, give_out, t...]
where the time goes in v4:
time: 233 us; the launch traced here: 229 us
  Pallas kernels  216 us (93%)
  other arithmetic  6.55 us (3%)
  local copies, waits for them, and re-layouts  6.13 us (3%)
    pallas_call x1, Pallas kernels, run_layer(): pl.pallas_call(functools.partial(layer_kernel, R, G, give_in, give_out, t...  216 us

profile of v4, /device:TPU:0, one launch (start us, length us, event | category | flops | bytes accessed | tf_op | source)
XLA Modules:
  0.0 229.1 jit_solution(4450273084733883455)
XLA Ops:
  0.7 215.7 %layer.1 = (f32[1088,256]{1,0:T(8,128)}, f32[1088,256]{1,0:T(8,128)}, bf16[3,136,1088]{2,1,0:T(8,128)(2,1)}, bf16[136,1088]{1,0:T(8,128)(2,1)}, bf16[4,136,1088]...) custom-call(s32[1,8]{1,0:T(1,128)} %refs_0_.1, ...), custom_call_target="tpu_custom_call" | custom-call | tf_op jit(solution)/shard_map/layer/pallas_call | solution.py:1501
  216.4 0.0 copy-start.4
  216.4 0.8 slice.34
  217.1 1.6 fusion
  218.7 0.7 reshape.39
  219.4 1.8 convert_bitcast_fusion.3
  221.2 0.0 copy-done.4
  221.2 0.0 copy-start.1
  221.2 1.4 convert_bitcast_fusion.2
  222.7 0.2 copy-done.1
  222.9 0.0 copy-start
  222.9 1.6 convert_bitcast_fusion.1
  224.4 0.3 copy-done
  224.7 0.0 copy-start.3
  224.7 1.7 convert_bitcast_fusion
  226.4 0.0 copy-done.3
  226.4 0.0 copy-start.2
  226.4 1.0 copy.33
  227.4 0.7 copy-done.2
  228.1 1.0 copy.34
Async XLA Ops:
  216.4 4.9 %copy-start.4 = (bf16[3,136,1088]{2,1,0:T(8,128)(2,1)S(1)}, bf16[3,136,1088]{2,1,0:T(8,128)(2,1)}, u32[]{:S(2)}) copy-start(bf16[3,136,1088]{2,1,0:T(8,128)(2,1)} %get-tuple-element.25) | copy-start | bytes 2663428
  221.2 1.6 copy-start.1
  222.9 1.8 copy-start
  224.7 1.7 copy-start.3
  226.4 1.6 copy-start.2

commit v5 on v4

--- a/solution.py
+++ b/solution.py
@@ -1400,7 +1400,7 @@
     Q = TEAM
     N = 4
     give_in = (6 * n // 17) // 8 * 8
-    give_out = (6 * n // 17) // 8 * 8
+    give_out = (5 * n // 17) // 8 * 8
     wide_out = n - give_out
     rounds = bits_of(R) + bits_of(G)
     deep = bits_of(R) - 2

time: 233 us -> 230 us (0.987)
  no operation moved by 1% of the time
where the time goes in v5:
time: 230 us; the launch traced here: 227 us
  Pallas kernels  214 us (93%)
  other arithmetic  6.55 us (3%)
  local copies, waits for them, and re-layouts  6.13 us (3%)
    pallas_call x1, Pallas kernels, run_layer(): pl.pallas_call(functools.partial(layer_kernel, R, G, give_in, give_out, t...  214 us

profile of v5, /device:TPU:0, one launch (start us, length us, event | category | flops | bytes accessed | tf_op | source)
XLA Modules:
  0.0 227.0 jit_solution(785413154376407107)
XLA Ops:
  0.7 213.6 %layer.1 = (f32[1088,256]{1,0:T(8,128)}, f32[1088,256]{1,0:T(8,128)}, bf16[3,136,1088]{2,1,0:T(8,128)(2,1)}, bf16[136,1088]{1,0:T(8,128)(2,1)}, bf16[4,136,1088]...) custom-call(s32[1,8]{1,0:T(1,128)} %refs_0_.1, ...), custom_call_target="tpu_custom_call" | custom-call | tf_op jit(solution)/shard_map/layer/pallas_call | solution.py:1501
  214.3 0.0 copy-start.4
  214.3 0.8 slice.34
  215.1 1.6 fusion
  216.6 0.7 reshape.39
  217.3 1.8 convert_bitcast_fusion.3
  219.1 0.0 copy-done.4
  219.1 0.0 copy-start.1
  219.1 1.4 convert_bitcast_fusion.2
  220.6 0.2 copy-done.1
  220.8 0.0 copy-start
  220.8 1.6 convert_bitcast_fusion.1
  222.3 0.3 copy-done
  222.6 0.0 copy-start.3
  222.6 1.7 convert_bitcast_fusion
  224.3 0.0 copy-done.3
  224.3 0.0 copy-start.2
  224.3 1.0 copy.33
  225.3 0.7 copy-done.2
  226.0 1.0 copy.34
Async XLA Ops:
  214.3 4.9 %copy-start.4 = (bf16[3,136,1088]{2,1,0:T(8,128)(2,1)S(1)}, bf16[3,136,1088]{2,1,0:T(8,128)(2,1)}, u32[]{:S(2)}) copy-start(bf16[3,136,1088]{2,1,0:T(8,128)(2,1)} %get-tuple-element.25) | copy-start | bytes 2663428
  219.1 1.6 copy-start.1
  220.8 1.8 copy-start
  222.6 1.7 copy-start.3
  224.3 1.6 copy-start.2
